TPU v7x, 128 devices: a whole 4x4x4 slice. The times are simulated.
128 devices in a mesh: zs: 8 (over z, core), ys: 16 (over y, x).
Axes of the slice: x: 4, y: 4, z: 4, core: 2. Of those that a mesh axis runs over, the one named last changes fastest.
Arguments:
- polarization: bfloat16 [2, 6, 256, 256, 1024], P(None, None, None, 'ys', 'zs'), may hold values from -6 to 6
- theta_index: int32 [512], replicated, may hold values from 0 to 179
- phi_index: int32 [512], replicated, may hold values from 0 to 359
Outputs:
- mueller: float32 [16, 512], replicated
All inputs are finite; a program needn't handle non-finite values.
Results may differ from a plain program's by a relative error of at most 0.0033.
Values sent between devices are 32-bit elements.
No kernel may reach another device: no remote copies, remote signals or barrier semaphores. Data moves between devices by JAX's collectives and lax.ppermute only.
A program may use at most 64 MiB of HBM per device.

v0:
```python
import math

import jax
import jax.numpy as jnp
from jax import lax
from jax.sharding import PartitionSpec as P

NTHETA = 180
NPHI = 360


wave_step = 0.6
pauli_set = (((1, 0), (0, 1)), ((1, 0), (0, -1)), ((0, 1), (1, 0)), ((0, -1j), (1j, 0)))


def copy_for_each(shard, axis):
    copies = jnp.broadcast_to(shard, (lax.axis_size(axis), *shard.shape))
    return lax.all_to_all(copies, axis, split_axis=0, concat_axis=0, tiled=True)


def of_everyone(shard, axis):
    return copy_for_each(shard, axis).sum(axis=0)


def angles(theta_index, phi_index):
    polar_angle = math.pi * (theta_index.astype(jnp.float32) + 0.5) / NTHETA
    azimuth = 2.0 * math.pi * phi_index.astype(jnp.float32) / NPHI
    return (polar_angle, azimuth)


def mueller_of(amplitude, polar_angle, azimuth):
    unit_theta = (
        jnp.cos(polar_angle) * jnp.cos(azimuth),
        jnp.cos(polar_angle) * jnp.sin(azimuth),
        -jnp.sin(polar_angle),
    )
    unit_phi = (-jnp.sin(azimuth), jnp.cos(azimuth))
    real_jones = [[None, None], [None, None]]
    imag_jones = [[None, None], [None, None]]
    for s, unit_vec in enumerate((unit_theta, unit_phi)):
        for p in range(2):
            real_sum = 0.0
            imag_sum = 0.0
            for c in range(len(unit_vec)):
                real_sum = real_sum + unit_vec[c] * amplitude[:, 3 * p + c]
                imag_sum = imag_sum + unit_vec[c] * amplitude[:, 6 + 3 * p + c]
            real_jones[s][p] = real_sum
            imag_jones[s][p] = imag_sum
    elements = []
    for i in range(4):
        for j in range(4):
            summed = 0.0
            for a in range(2):
                for b in range(2):
                    for c in range(2):
                        for e in range(2):
                            weight = complex(pauli_set[i][a][b]) * complex(pauli_set[j][c][e])
                            if weight == 0:
                                continue
                            z_real = (
                                real_jones[b][c] * real_jones[a][e]
                                + imag_jones[b][c] * imag_jones[a][e]
                            )
                            z_imag = (
                                imag_jones[b][c] * real_jones[a][e]
                                - real_jones[b][c] * imag_jones[a][e]
                            )
                            summed = summed + weight.real * z_real - weight.imag * z_imag
            elements.append(0.5 * summed)
    return jnp.stack(elements)


def body(polarization, theta_index, phi_index):
    halves, components, cells_x, cells_y, cells_z = polarization.shape
    count_y = lax.axis_size("ys")
    count_z = lax.axis_size("zs")
    total_y = cells_y * count_y
    total_z = cells_z * count_z
    polar_angle, azimuth = angles(theta_index, phi_index)
    unit_x = jnp.sin(polar_angle) * jnp.cos(azimuth)
    unit_y = jnp.sin(polar_angle) * jnp.sin(azimuth)
    unit_z = jnp.cos(polar_angle)
    pos_x = (jnp.arange(cells_x) - cells_x // 2).astype(jnp.float32)
    pos_y = (lax.axis_index("ys") * cells_y + jnp.arange(cells_y) - total_y // 2).astype(
        jnp.float32
    )
    pos_z = (lax.axis_index("zs") * cells_z + jnp.arange(cells_z) - total_z // 2).astype(
        jnp.float32
    )
    flattened = polarization.reshape(halves, components, cells_x, cells_y * cells_z)
    scaling = 1.0 / math.sqrt(cells_x * total_y * total_z)
    directions = theta_index.shape[0]
    block_size = 64

    def one_block(first_row):
        bx = lax.dynamic_slice_in_dim(unit_x, first_row, block_size)
        by = lax.dynamic_slice_in_dim(unit_y, first_row, block_size)
        bz = lax.dynamic_slice_in_dim(unit_z, first_row, block_size)
        phase_x = wave_step * bx[:, None] * pos_x[None, :]
        tables = jnp.stack([jnp.cos(phase_x), jnp.sin(phase_x)]).astype(jnp.bfloat16)
        summed = jnp.einsum(
            "tdx,rcxq->tdrcq", tables, flattened, preferred_element_type=jnp.float32
        )
        real_x = summed[0, :, 0] + summed[1, :, 1]
        imag_x = summed[0, :, 1] - summed[1, :, 0]
        phase_yz = wave_step * (
            by[:, None, None] * pos_y[None, :, None] + bz[:, None, None] * pos_z[None, None, :]
        )
        phase_yz = phase_yz.reshape(block_size, cells_y * cells_z)
        cos_yz = jnp.cos(phase_yz)[:, None, :]
        sin_yz = jnp.sin(phase_yz)[:, None, :]
        real_part = jnp.sum(real_x * cos_yz + imag_x * sin_yz, axis=-1)
        imag_part = jnp.sum(imag_x * cos_yz - real_x * sin_yz, axis=-1)
        return jnp.concatenate([real_part, imag_part], axis=1) * scaling

    def amplitudes(start_row, row_count):
        if row_count % block_size == 0:
            firsts = (start_row + jnp.arange(row_count // block_size) * block_size).astype(
                jnp.int32
            )
            return lax.map(one_block, firsts).reshape(row_count, 12)
        block_count = min(row_count // block_size + 2, directions // block_size)
        cover_start = jnp.clip(
            start_row // block_size * block_size, 0, directions - block_count * block_size
        ).astype(jnp.int32)
        firsts = (cover_start + jnp.arange(block_count) * block_size).astype(jnp.int32)
        covered = lax.map(one_block, firsts).reshape(block_count * block_size, 12)
        return lax.dynamic_slice_in_dim(
            covered, (start_row - cover_start).astype(jnp.int32), row_count
        )

    partial_rows = amplitudes(0, directions)
    complete = of_everyone(of_everyone(partial_rows, "zs"), "ys")
    return mueller_of(complete, polar_angle, azimuth)


def solution(mesh):
    return jax.shard_map(
        body,
        mesh=mesh,
        in_specs=(P(None, None, None, "ys", "zs"), P(), P()),
        out_specs=P(),
        check_vma=False,
    )
```

profile of v0, /device:TPU:0, one launch (start us, length us, event | category | flops | bytes accessed | tf_op | source)
XLA Modules:
  0.0 160.8 jit_solution(15696974517515432163)
XLA Ops:
  0.0 19.3 %reshape.209 = bf16[2,6,256,2048]{3,2,1,0:T(8,128)(2,1)} reshape(bf16[2,6,256,16,128]{4,3,2,1,0:T(8,128)(2,1)} %param.5) | data formatting | bytes 25165824 | tf_op jit(solution)/shard_map/reshape | solution.py:90
  19.4 108.9 %while.11 = (s32[]{:T(128)}, f32[8,64,12]{1,0,2:T(8,128)S(1)}, s32[8]{0:T(128)S(1)}, f32[512]{0:T(512)S(1)}, bf16[2,6,256,2048]{3,2,1,0:T(8,128)(2,1)}, /*index=...) while((s32[]{:T(128)}, f32[8,64,12]{1,0,2:T(8,128)S(1)}, ...), condition=%wide.region_3.4_spmd.clone, body=%wide.region_0.3_spmd.clone.sunk | while | flops 1618930432 | bytes 42175036 | solution.py:121
  19.4 0.6 dynamic_slice.23
  22.3 1.9 %fusion.36 = (f32[64,16,128]{2,1,0:T(8,128)S(1)}, f32[64,16,128]{2,1,0:T(8,128)S(1)}) fusion(f32[64,128]{1,0:T(8,128)S(1)} %broadcast_multiply_fusion.4, f32[64,16]{1,0:T(8,128)S(1)} %broadcast_multiply_fusion.5), kind=kLoop, calls=%fused_computation.15.clone.1 | loop fusion | flops 262144 | bytes 1085440 | tf_op jit(solution)/shard_map/while/body/eval_jaxpr/cos | solution.py:110
  24.9 6.5 %fusion.38 = f32[2,64,2,6,2048]{4,1,3,2,0:T(8,128)S(1)} fusion(bf16[2,6,256,2048]{3,2,1,0:T(8,128)(2,1)} %get-tuple-element.303, bf16[1,64,256]{2,1,0:T(8,128)(2,1)S(1)} %get-tuple-element.271, bf16[1,64,256]{2,1,0:T(8,128)(2,1)S(1)} %get-tuple-element.272), kind=kOutput, calls=%fused_computation.3.clone.1 | convolution fusion | flops 1610743808 | bytes 25231360 | tf_op jit(solution)/shard_map/while/body/eval_jaxpr/tdx,rcxq->tdrcq/dot_general | solution.py:101
  31.4 1.6 add_reduce_fusion.2
  33.0 0.6 dynamic_slice.23
  35.9 1.9 %fusion.36 = (f32[64,16,128]{2,1,0:T(8,128)S(1)}, f32[64,16,128]{2,1,0:T(8,128)S(1)}) fusion(f32[64,128]{1,0:T(8,128)S(1)} %broadcast_multiply_fusion.4, f32[64,16]{1,0:T(8,128)S(1)} %broadcast_multiply_fusion.5), kind=kLoop, calls=%fused_computation.15.clone.1 | loop fusion | flops 262144 | bytes 1085440 | tf_op jit(solution)/shard_map/while/body/eval_jaxpr/cos | solution.py:110
  38.5 6.5 %fusion.38 = f32[2,64,2,6,2048]{4,1,3,2,0:T(8,128)S(1)} fusion(bf16[2,6,256,2048]{3,2,1,0:T(8,128)(2,1)} %get-tuple-element.303, bf16[1,64,256]{2,1,0:T(8,128)(2,1)S(1)} %get-tuple-element.271, bf16[1,64,256]{2,1,0:T(8,128)(2,1)S(1)} %get-tuple-element.272), kind=kOutput, calls=%fused_computation.3.clone.1 | convolution fusion | flops 1610743808 | bytes 25231360 | tf_op jit(solution)/shard_map/while/body/eval_jaxpr/tdx,rcxq->tdrcq/dot_general | solution.py:101
  45.0 1.6 add_reduce_fusion.2
  46.7 0.6 dynamic_slice.23
  49.5 1.9 %fusion.36 = (f32[64,16,128]{2,1,0:T(8,128)S(1)}, f32[64,16,128]{2,1,0:T(8,128)S(1)}) fusion(f32[64,128]{1,0:T(8,128)S(1)} %broadcast_multiply_fusion.4, f32[64,16]{1,0:T(8,128)S(1)} %broadcast_multiply_fusion.5), kind=kLoop, calls=%fused_computation.15.clone.1 | loop fusion | flops 262144 | bytes 1085440 | tf_op jit(solution)/shard_map/while/body/eval_jaxpr/cos | solution.py:110
  52.1 6.5 %fusion.38 = f32[2,64,2,6,2048]{4,1,3,2,0:T(8,128)S(1)} fusion(bf16[2,6,256,2048]{3,2,1,0:T(8,128)(2,1)} %get-tuple-element.303, bf16[1,64,256]{2,1,0:T(8,128)(2,1)S(1)} %get-tuple-element.271, bf16[1,64,256]{2,1,0:T(8,128)(2,1)S(1)} %get-tuple-element.272), kind=kOutput, calls=%fused_computation.3.clone.1 | convolution fusion | flops 1610743808 | bytes 25231360 | tf_op jit(solution)/shard_map/while/body/eval_jaxpr/tdx,rcxq->tdrcq/dot_general | solution.py:101
  58.6 1.6 add_reduce_fusion.2
  63.1 1.9 %fusion.36 = (f32[64,16,128]{2,1,0:T(8,128)S(1)}, f32[64,16,128]{2,1,0:T(8,128)S(1)}) fusion(f32[64,128]{1,0:T(8,128)S(1)} %broadcast_multiply_fusion.4, f32[64,16]{1,0:T(8,128)S(1)} %broadcast_multiply_fusion.5), kind=kLoop, calls=%fused_computation.15.clone.1 | loop fusion | flops 262144 | bytes 1085440 | tf_op jit(solution)/shard_map/while/body/eval_jaxpr/cos | solution.py:110
  65.8 6.5 %fusion.38 = f32[2,64,2,6,2048]{4,1,3,2,0:T(8,128)S(1)} fusion(bf16[2,6,256,2048]{3,2,1,0:T(8,128)(2,1)} %get-tuple-element.303, bf16[1,64,256]{2,1,0:T(8,128)(2,1)S(1)} %get-tuple-element.271, bf16[1,64,256]{2,1,0:T(8,128)(2,1)S(1)} %get-tuple-element.272), kind=kOutput, calls=%fused_computation.3.clone.1 | convolution fusion | flops 1610743808 | bytes 25231360 | tf_op jit(solution)/shard_map/while/body/eval_jaxpr/tdx,rcxq->tdrcq/dot_general | solution.py:101
  72.2 1.6 add_reduce_fusion.2
  76.7 1.9 %fusion.36 = (f32[64,16,128]{2,1,0:T(8,128)S(1)}, f32[64,16,128]{2,1,0:T(8,128)S(1)}) fusion(f32[64,128]{1,0:T(8,128)S(1)} %broadcast_multiply_fusion.4, f32[64,16]{1,0:T(8,128)S(1)} %broadcast_multiply_fusion.5), kind=kLoop, calls=%fused_computation.15.clone.1 | loop fusion | flops 262144 | bytes 1085440 | tf_op jit(solution)/shard_map/while/body/eval_jaxpr/cos | solution.py:110
  79.4 6.5 %fusion.38 = f32[2,64,2,6,2048]{4,1,3,2,0:T(8,128)S(1)} fusion(bf16[2,6,256,2048]{3,2,1,0:T(8,128)(2,1)} %get-tuple-element.303, bf16[1,64,256]{2,1,0:T(8,128)(2,1)S(1)} %get-tuple-element.271, bf16[1,64,256]{2,1,0:T(8,128)(2,1)S(1)} %get-tuple-element.272), kind=kOutput, calls=%fused_computation.3.clone.1 | convolution fusion | flops 1610743808 | bytes 25231360 | tf_op jit(solution)/shard_map/while/body/eval_jaxpr/tdx,rcxq->tdrcq/dot_general | solution.py:101
  85.8 1.6 add_reduce_fusion.2
  90.3 1.9 %fusion.36 = (f32[64,16,128]{2,1,0:T(8,128)S(1)}, f32[64,16,128]{2,1,0:T(8,128)S(1)}) fusion(f32[64,128]{1,0:T(8,128)S(1)} %broadcast_multiply_fusion.4, f32[64,16]{1,0:T(8,128)S(1)} %broadcast_multiply_fusion.5), kind=kLoop, calls=%fused_computation.15.clone.1 | loop fusion | flops 262144 | bytes 1085440 | tf_op jit(solution)/shard_map/while/body/eval_jaxpr/cos | solution.py:110
  93.0 6.5 %fusion.38 = f32[2,64,2,6,2048]{4,1,3,2,0:T(8,128)S(1)} fusion(bf16[2,6,256,2048]{3,2,1,0:T(8,128)(2,1)} %get-tuple-element.303, bf16[1,64,256]{2,1,0:T(8,128)(2,1)S(1)} %get-tuple-element.271, bf16[1,64,256]{2,1,0:T(8,128)(2,1)S(1)} %get-tuple-element.272), kind=kOutput, calls=%fused_computation.3.clone.1 | convolution fusion | flops 1610743808 | bytes 25231360 | tf_op jit(solution)/shard_map/while/body/eval_jaxpr/tdx,rcxq->tdrcq/dot_general | solution.py:101
  99.4 1.6 add_reduce_fusion.2
  103.9 1.9 %fusion.36 = (f32[64,16,128]{2,1,0:T(8,128)S(1)}, f32[64,16,128]{2,1,0:T(8,128)S(1)}) fusion(f32[64,128]{1,0:T(8,128)S(1)} %broadcast_multiply_fusion.4, f32[64,16]{1,0:T(8,128)S(1)} %broadcast_multiply_fusion.5), kind=kLoop, calls=%fused_computation.15.clone.1 | loop fusion | flops 262144 | bytes 1085440 | tf_op jit(solution)/shard_map/while/body/eval_jaxpr/cos | solution.py:110
  106.6 6.5 %fusion.38 = f32[2,64,2,6,2048]{4,1,3,2,0:T(8,128)S(1)} fusion(bf16[2,6,256,2048]{3,2,1,0:T(8,128)(2,1)} %get-tuple-element.303, bf16[1,64,256]{2,1,0:T(8,128)(2,1)S(1)} %get-tuple-element.271, bf16[1,64,256]{2,1,0:T(8,128)(2,1)S(1)} %get-tuple-element.272), kind=kOutput, calls=%fused_computation.3.clone.1 | convolution fusion | flops 1610743808 | bytes 25231360 | tf_op jit(solution)/shard_map/while/body/eval_jaxpr/tdx,rcxq->tdrcq/dot_general | solution.py:101
  113.1 1.6 add_reduce_fusion.2
  117.5 1.9 %fusion.36 = (f32[64,16,128]{2,1,0:T(8,128)S(1)}, f32[64,16,128]{2,1,0:T(8,128)S(1)}) fusion(f32[64,128]{1,0:T(8,128)S(1)} %broadcast_multiply_fusion.4, f32[64,16]{1,0:T(8,128)S(1)} %broadcast_multiply_fusion.5), kind=kLoop, calls=%fused_computation.15.clone.1 | loop fusion | flops 262144 | bytes 1085440 | tf_op jit(solution)/shard_map/while/body/eval_jaxpr/cos | solution.py:110
  120.2 6.5 %fusion.38 = f32[2,64,2,6,2048]{4,1,3,2,0:T(8,128)S(1)} fusion(bf16[2,6,256,2048]{3,2,1,0:T(8,128)(2,1)} %get-tuple-element.303, bf16[1,64,256]{2,1,0:T(8,128)(2,1)S(1)} %get-tuple-element.271, bf16[1,64,256]{2,1,0:T(8,128)(2,1)S(1)} %get-tuple-element.272), kind=kOutput, calls=%fused_computation.3.clone.1 | convolution fusion | flops 1610743808 | bytes 25231360 | tf_op jit(solution)/shard_map/while/body/eval_jaxpr/tdx,rcxq->tdrcq/dot_general | solution.py:101
  126.7 1.6 add_reduce_fusion.2
  128.4 12.7 %all_to_all.10 = f32[8,512,12]{1,2,0:T(8,128)S(1)} all-to-all(f32[8,512,12]{1,2,0:T(8,128)S(1)} %broadcast_in_dim.8), channel_id=1, replica_groups=mesh['zs'=8,'ys'=16] {'zs'}, dimensions={0} | all-to-all | bytes 393216 | tf_op jit(solution)/shard_map/all_to_all | solution.py:18
  141.2 18.0 %all_to_all.11 = f32[16,512,12]{1,2,0:T(8,128)S(1)} all-to-all(f32[16,512,12]{1,2,0:T(8,128)S(1)} %broadcast_in_dim.9), channel_id=1, replica_groups=mesh['zs'=8,'ys'=16] {'ys'}, dimensions={0} | all-to-all | bytes 786432 | tf_op jit(solution)/shard_map/all_to_all | solution.py:18
  159.5 1.3 stack.73
  (128 shorter events, 12.4 us)
Async XLA Ops:
  0.0 19.4 %copy-start = (s32[512]{0:T(512)S(1)}, s32[512]{0:T(512)}, u32[]{:S(2)}) copy-start(s32[512]{0:T(512)} %param.7) | copy-start | bytes 6148
  0.0 19.4 %copy-start.1 = (s32[512]{0:T(512)S(1)}, s32[512]{0:T(512)}, u32[]{:S(2)}) copy-start(s32[512]{0:T(512)} %param.6) | copy-start | bytes 6148
where the time goes:
time: 162 us; the launch traced here: 161 us
  matrix products  51.6 us (32%)
  other arithmetic  32.6 us (20%)
  blocking collectives  30.7 us (19%)
  local copies, waits for them, and re-layouts  30.1 us (19%)
  loops' own time  15.7 us (10%)
    dot_general x8, matrix products, one_block(): jnp.einsum('tdx,rcxq->tdrcq', tables, flattened, preferred_element_type=j...  51.6 us
    all_to_all x2, blocking collectives, copy_for_each(): return lax.all_to_all(copies, axis, split_axis=0, concat_axis=0, tiled=True)  30.7 us
    reshape x1, local copies, waits for them, and re-layouts, body(): polarization.reshape(halves, components, cells_x, cells_y * cells_z)  19.3 us
    another operation x1, loops' own time, amplitudes(): return lax.map(one_block, firsts).reshape(row_count, 12)  15.7 us
    cos x8, other arithmetic, one_block(): cos_yz = jnp.cos(phase_yz)[:, None, :]  15.3 us
    reduce_sum x8, other arithmetic, one_block(): real_part = jnp.sum(real_x * cos_yz + imag_x * sin_yz, axis=-1)  12.5 us
    dynamic_slice x8, local copies, waits for them, and re-layouts, amplitudes(): return lax.map(one_block, firsts).reshape(row_count, 12)  4.96 us

commit v1 on v0

v1 whole, which is shorter than its diff:
```python
import functools, math
import jax, jax.numpy as jnp
from jax import lax
from jax.experimental import pallas as pl
from jax.experimental.pallas import tpu as pltpu
from jax.sharding import PartitionSpec as P

WAVE = 0.6
XB = 16
ORIENT = 2
AXES = True

def sincos_turns(u):
    r = u - jnp.floor(u + 0.5)
    t = r * r
    w = 2.0 * math.pi
    cos_k = [(-1) ** n * w ** (2 * n) / math.factorial(2 * n) for n in range(11)]
    sin_k = [(-1) ** n * w ** (2 * n + 1) / math.factorial(2 * n + 1) for n in range(10)]
    c = jnp.full_like(t, cos_k[-1])
    for k in cos_k[-2::-1]:
        c = c * t + k
    s = jnp.full_like(t, sin_k[-1])
    for k in sin_k[-2::-1]:
        s = s * t + k
    return c, s * r

def kernel(th_ref, ph_ref, p_hbm, out_ref, pv, w_ref, t_ref, acc_ref, tc_ref, ts_ref, sems):
    _, _, gx, ny, nz = pv.shape
    half = gx // 2
    dirs = th_ref.shape[1]
    f32, bf16 = jnp.float32, jnp.bfloat16
    nfold = half // XB - 1
    kb = XB * ny
    pieces = []
    for i in range(nfold):
        pieces.append([(half + 1 + XB * i, XB), (half - XB * (i + 1), XB)])
    pieces.append([(half, 1), (gx - XB + 1, XB - 1)])
    pieces.append([(0, XB)])
    copies = []
    n = 0
    for group in pieces:
        made = []
        for x0, cnt in group:
            made.append(pltpu.make_async_copy(p_hbm.at[:, :, pl.ds(x0, cnt)], pv.at[:, :, pl.ds(x0, cnt)], sems.at[n]))
            n += 1
        copies.append(made)
    ahead = 4
    for made in copies[:ahead]:
        for cp in made: cp.start()

    ct, st = sincos_turns((th_ref[...].astype(f32) + 0.5) * (1.0 / 360.0))
    cp_, sp_ = sincos_turns(ph_ref[...].astype(f32) * (1.0 / 360.0))
    scale = WAVE / (2.0 * math.pi)
    ux, uy, uz = scale * (st * cp_), scale * (st * sp_), scale * ct
    rows = tc_ref.shape[0]
    px = lax.broadcasted_iota(jnp.int32, (rows, dirs), 0).astype(f32)
    c, s = sincos_turns(px * ux)
    tc_ref[...] = c.astype(bf16).astype(f32)
    ts_ref[...] = s.astype(bf16).astype(f32)
    qy = lax.broadcasted_iota(jnp.int32, (ny, dirs), 0).astype(f32) - (ny - 1) / 2.0
    cy, sy = sincos_turns(qy * uy)
    flip_idx = 7 - lax.broadcasted_iota(jnp.int32, (2, 6, ny // 8, 8, nz), 3)

    def make_tables(step, slot):
        for xl in range(XB):
            if step < nfold: px = 1 + XB * step + xl
            elif step == nfold: px = 0 if xl == 0 else half - XB + xl
            else: px = xl - half
            tc = tc_ref[pl.ds(abs(px), 1), :]
            ts = ts_ref[pl.ds(abs(px), 1), :]
            if px < 0: ts = -ts
            k = xl * ny
            t_ref[slot, pl.ds(k, ny), :] = (tc * cy - ts * sy).astype(bf16)
            t_ref[slot, pl.ds(kb + k, ny), :] = (ts * cy + tc * sy).astype(bf16)

    def fill(step, slot):
        for xl in range(XB):
            k = xl * ny
            if step < nfold:
                off = 1 + XB * step + xl
                p = pv[:, :, half + off]
                m = pv[:, :, half - off].astype(f32).reshape(2, 6, ny // 8, 8, nz)
                m = jnp.take_along_axis(m, flip_idx, axis=3)
                m = jnp.concatenate([m[:, :, 1:2], m[:, :, 0:1]], axis=2).reshape(2, 6, ny, nz).astype(bf16)
                e = p + m
                er, ei = e[0], e[1]
                oi = p[1] - m[1]
                nor = m[0] - p[0]
            else:
                x = (half if xl == 0 else gx - XB + xl) if step == nfold else xl
                p = pv[:, :, x]
                er, ei, oi, nor = p[0], p[1], p[1], -p[0]
            w_ref[slot, 0:6, pl.ds(k, ny), :] = er
            w_ref[slot, 6:12, pl.ds(k, ny), :] = ei
            w_ref[slot, 0:6, pl.ds(kb + k, ny), :] = oi
            w_ref[slot, 6:12, pl.ds(kb + k, ny), :] = nor

    def multiply(step, slot):
        w = jnp.concatenate([w_ref[slot, j] for j in range(12)], axis=1)
        t = t_ref[slot]
        if ORIENT == 2:
            g = lax.dot_general(w, t, (((0,), (0,)), ((), ())), preferred_element_type=f32)
        else:
            g = lax.dot_general(t, w, (((0,), (0,)), ((), ())), preferred_element_type=f32)
        if step == 0: acc_ref[...] = g
        else: acc_ref[...] += g

    steps = len(copies)
    make_tables(0, 0)
    for cp in copies[0]: cp.wait()
    fill(0, 0)
    for step in range(steps):
        if step + ahead < steps:
            for cp in copies[step + ahead]: cp.start()
        if step + 1 < steps:
            for cp in copies[step + 1]: cp.wait()
            make_tables(step + 1, (step + 1) % 2)
            fill(step + 1, (step + 1) % 2)
        multiply(step, step % 2)

    if AXES:
        ys, total_y = lax.axis_index("ys"), ny * lax.axis_size("ys")
        zs, total_z = lax.axis_index("zs"), nz * lax.axis_size("zs")
    else:
        ys, total_y, zs, total_z = 3, 256, 2, 1024
    cyg = jnp.float32(ys * ny - total_y // 2) + (ny - 1) / 2.0
    z0 = jnp.float32(zs * nz - total_z // 2)
    qz = lax.broadcasted_iota(jnp.int32, (nz, dirs), 0).astype(f32) + z0
    cz, sz = sincos_turns(qz * uz + cyg * uy)
    total = 1.0 / math.sqrt(gx * total_y * total_z)
    outs = [None] * 12
    for c in range(6):
        if ORIENT == 2:
            re = acc_ref[pl.ds(c * nz, nz), :]
            im = acc_ref[pl.ds((6 + c) * nz, nz), :]
            outs[c] = jnp.sum(re * cz + im * sz, axis=0, keepdims=True) * total
            outs[6 + c] = jnp.sum(im * cz - re * sz, axis=0, keepdims=True) * total
    result = jnp.concatenate(outs, axis=0)
    for i in range(out_ref.shape[0]):
        out_ref[i] = result

def far_field(p, th, ph, copies):
    dirs = th.shape[1]
    r, ncomp, gx, ny, nz = p.shape
    return pl.pallas_call(
        kernel,
        name="far_field",
        out_shape=jax.ShapeDtypeStruct((copies, 12, dirs), jnp.float32),
        in_specs=[pl.BlockSpec(memory_space=pltpu.VMEM),
                  pl.BlockSpec(memory_space=pltpu.VMEM), pl.BlockSpec(memory_space=pl.ANY)],
        out_specs=pl.BlockSpec(memory_space=pltpu.VMEM),
        scratch_shapes=[
            pltpu.VMEM((r, ncomp, gx, ny, nz), jnp.bfloat16),
            pltpu.VMEM((2, 12, 2 * XB * ny, nz), jnp.bfloat16),
            pltpu.VMEM((2, 2 * XB * ny, dirs), jnp.bfloat16),
            pltpu.VMEM((12 * nz, dirs), jnp.float32),
            pltpu.VMEM((gx // 2 + 8, dirs), jnp.float32),
            pltpu.VMEM((gx // 2 + 8, dirs), jnp.float32),
            pltpu.SemaphoreType.DMA((2 * (gx // 2 // XB) + 1,)),
        ],
        compiler_params=pltpu.CompilerParams(vmem_limit_bytes=50 * 2**20),
    )(th, ph, p)


def sum_kernel(x_ref, o_ref):
    total = x_ref[0]
    for i in range(1, x_ref.shape[0]):
        total = total + x_ref[i]
    for i in range(o_ref.shape[0]):
        o_ref[i] = total


def sum_copies(x, copies):
    return pl.pallas_call(
        sum_kernel,
        name="sum_copies",
        out_shape=jax.ShapeDtypeStruct((copies, *x.shape[1:]), jnp.float32),
    )(x)


PAULI = (((1, 0), (0, 1)), ((1, 0), (0, -1)), ((0, 1), (1, 0)), ((0, -1j), (1j, 0)))


def mueller_kernel(x_ref, th_ref, ph_ref, o_ref):
    amplitude = x_ref[0]
    for i in range(1, x_ref.shape[0]):
        amplitude = amplitude + x_ref[i]
    ct, st = sincos_turns((th_ref[...].astype(jnp.float32) + 0.5) * (1.0 / 360.0))
    cp, sp = sincos_turns(ph_ref[...].astype(jnp.float32) * (1.0 / 360.0))
    units = ((ct * cp, ct * sp, -st), (-sp, cp))
    re = [[None, None], [None, None]]
    im = [[None, None], [None, None]]
    for s, unit in enumerate(units):
        for p in range(2):
            a = b = 0.0
            for c, u in enumerate(unit):
                a = a + u * amplitude[3 * p + c : 3 * p + c + 1]
                b = b + u * amplitude[6 + 3 * p + c : 7 + 3 * p + c]
            re[s][p], im[s][p] = a, b
    known = {}

    def product(b, c, a, e):
        if (b, c, a, e) not in known:
            known[b, c, a, e] = (re[b][c] * re[a][e] + im[b][c] * im[a][e],
                                 im[b][c] * re[a][e] - re[b][c] * im[a][e])
        return known[b, c, a, e]

    for i in range(4):
        for j in range(4):
            total = 0.0
            for a in range(2):
                for b in range(2):
                    for c in range(2):
                        for e in range(2):
                            weight = complex(PAULI[i][a][b]) * complex(PAULI[j][c][e])
                            if weight == 0:
                                continue
                            zr, zi = product(b, c, a, e)
                            if weight.real:
                                total = total + weight.real * zr
                            if weight.imag:
                                total = total - weight.imag * zi
            o_ref[4 * i + j : 4 * i + j + 1, :] = 0.5 * total


def mueller(x, th, ph):
    return pl.pallas_call(
        mueller_kernel,
        name="mueller",
        out_shape=jax.ShapeDtypeStruct((16, x.shape[2]), jnp.float32),
    )(x, th, ph)


def body(polarization, theta_index, phi_index):
    dirs = theta_index.shape[0]
    th, ph = theta_index.reshape(1, dirs), phi_index.reshape(1, dirs)
    copies = far_field(polarization, th, ph, lax.axis_size("zs"))
    copies = lax.all_to_all(copies, "zs", split_axis=0, concat_axis=0, tiled=True)
    copies = sum_copies(copies, lax.axis_size("ys"))
    copies = lax.all_to_all(copies, "ys", split_axis=0, concat_axis=0, tiled=True)
    return mueller(copies, th, ph)


def solution(mesh):
    return jax.shard_map(
        body,
        mesh=mesh,
        in_specs=(P(None, None, None, "ys", "zs"), P(), P()),
        out_specs=P(),
        check_vma=False,
    )
```

time: 162 us -> 52.1 us (0.32)
  matrix products: 51.6 us -> 0 us
  other arithmetic: 32.6 us -> 0 us
  local copies, waits for them, and re-layouts: 30.1 us -> 1.36 us
  Pallas kernels: 0 us -> 19.3 us
  loops' own time: 15.7 us -> 0 us
    dot_general x8 -> x0, matrix products: 51.6 us -> none  [one_block(): jnp.einsum('tdx,rcxq->tdrcq', tables, flattened, preferred_element_type=j...]
    reshape x2 -> x0, local copies, waits for them, and re-layouts: 19.4 us -> none  [the longest x1 19.3 us: body(): polarization.reshape(halves, components, cells_x, cells_y * cells_z)]
    pallas_call x0 -> x3, Pallas kernels: none -> 19.3 us  [the longest x1 15.8 us: far_field(): pl.pallas_call(kernel, name='far_field', out_shape=jax.ShapeDtypeStruct((...]
    another operation x1 -> x0, loops' own time: 15.7 us -> none  [amplitudes(): return lax.map(one_block, firsts).reshape(row_count, 12)]
    cos x8 -> x0, other arithmetic: 15.3 us -> none  [one_block(): cos_yz = jnp.cos(phase_yz)[:, None, :]]
    reduce_sum x10 -> x0, other arithmetic: 12.6 us -> none  [the longest x8 12.5 us: one_block(): real_part = jnp.sum(real_x * cos_yz + imag_x * sin_yz, axis=-1)]
    dynamic_slice x24 -> x0, local copies, waits for them, and re-layouts: 6.16 us -> none  [the longest x8 4.96 us: amplitudes(): return lax.map(one_block, firsts).reshape(row_count, 12)]
    sin x8 -> x0, local copies, waits for them, and re-layouts: 2.74 us -> none  [one_block(): sin_yz = jnp.sin(phase_yz)[:, None, :]]
where the time goes in v1:
time: 52.1 us; the launch traced here: 51.8 us
  blocking collectives  31.1 us (60%)
  Pallas kernels  19.3 us (37%)
  local copies, waits for them, and re-layouts  1.36 us (3%)
    all_to_all x1, blocking collectives, body(): lax.all_to_all(copies, 'ys', split_axis=0, concat_axis=0, tiled=True)  18.3 us
    pallas_call x1, Pallas kernels, far_field(): pl.pallas_call(kernel, name='far_field', out_shape=jax.ShapeDtypeStruct((...  15.8 us
    all_to_all x1, blocking collectives, body(): lax.all_to_all(copies, 'zs', split_axis=0, concat_axis=0, tiled=True)  12.8 us
    pallas_call x1, Pallas kernels, sum_copies(): pl.pallas_call(sum_kernel, name='sum_copies', out_shape=jax.ShapeDtypeStr...  1.79 us
    pallas_call x1, Pallas kernels, mueller(): pl.pallas_call(mueller_kernel, name='mueller', out_shape=jax.ShapeDtypeSt...  1.74 us
    unnamed x4, local copies, waits for them, and re-layouts  1.36 us

profile of v1, /device:TPU:0, one launch (start us, length us, event | category | flops | bytes accessed | tf_op | source)
XLA Modules:
  0.0 51.8 jit_solution(1988339283016138601)
XLA Ops:
  0.0 0.0 copy-start
  0.0 0.7 %copy-done = s32[512]{0:T(512)S(1)} copy-done((s32[512]{0:T(512)S(1)}, s32[512]{0:T(512)}, u32[]{:S(2)}) %copy-start) | copy-done | bytes 2072
  0.7 0.0 copy-start.1
  0.7 0.7 %copy-done.1 = s32[512]{0:T(512)S(1)} copy-done((s32[512]{0:T(512)S(1)}, s32[512]{0:T(512)}, u32[]{:S(2)}) %copy-start.1) | copy-done | bytes 2072
  1.4 15.8 %far_field.1 = f32[8,12,512]{2,1,0:T(8,128)S(1)} custom-call(s32[1,512]{1,0:T(1,128)S(1)} %bitcast.3, s32[1,512]{1,0:T(1,128)S(1)} %bitcast.5, bf16[2,6,256,16,128]{4,3,2,1,0:T(8,128)(2,1)} %p_hbm.1), custom_call_target="tpu_custom_call" | custom-call | tf_op jit(solution)/shard_map/far_field/pallas_call | solution.py:145
  17.1 12.8 %all_to_all.10.x_ref = f32[8,12,512]{2,1,0:T(8,128)} all-to-all(f32[8,12,512]{2,1,0:T(8,128)S(1)} %far_field.1), channel_id=1, replica_groups=mesh['zs'=8,'ys'=16] {'zs'}, dimensions={0} | all-to-all | bytes 393216 | tf_op jit(solution)/shard_map/all_to_all | solution.py:238
  30.0 1.8 %sum_copies.1 = f32[16,12,512]{2,1,0:T(8,128)} custom-call(f32[8,12,512]{2,1,0:T(8,128)} %all_to_all.10.x_ref), custom_call_target="tpu_custom_call" | custom-call | tf_op jit(solution)/shard_map/sum_copies/pallas_call | solution.py:174
  31.8 18.3 %all_to_all.11.x_ref = f32[16,12,512]{2,1,0:T(8,128)} all-to-all(f32[16,12,512]{2,1,0:T(8,128)} %sum_copies.1), channel_id=1, replica_groups=mesh['zs'=8,'ys'=16] {'ys'}, dimensions={0} | all-to-all | bytes 786432 | tf_op jit(solution)/shard_map/all_to_all | solution.py:240
  50.1 1.7 %mueller.1 = f32[16,512]{1,0:T(8,128)} custom-call(f32[16,12,512]{2,1,0:T(8,128)} %all_to_all.11.x_ref, s32[1,512]{1,0:T(1,128)} %bitcast.2, s32[1,512]{1,0:T(1,128)} %bitcast.4), custom_call_target="tpu_custom_call" | custom-call | tf_op jit(solution)/shard_map/mueller/pallas_call | solution.py:227
Async XLA Ops:
  0.0 0.7 %copy-start = (s32[512]{0:T(512)S(1)}, s32[512]{0:T(512)}, u32[]{:S(2)}) copy-start(s32[512]{0:T(512)} %param.4) | copy-start | bytes 6148
  0.7 0.7 %copy-start.1 = (s32[512]{0:T(512)S(1)}, s32[512]{0:T(512)}, u32[]{:S(2)}) copy-start(s32[512]{0:T(512)} %param.5) | copy-start | bytes 6148

commit v2 on v1

v2 whole, which is shorter than its diff:
```python
import math

import jax
import jax.numpy as jnp
from jax import lax
from jax.experimental import pallas as pl
from jax.experimental.pallas import tpu as pltpu
from jax.sharding import PartitionSpec as P

WAVE = 0.6
NTHETA = 180
NPHI = 360
XB = 16
GROUPS = (1, 2, 3, 3)
AHEAD = 9


def sincos_turns(u):
    r = u - jnp.floor(u + 0.5)
    t = r * r
    w = 2.0 * math.pi
    cos_k = [(-1) ** n * w ** (2 * n) / math.factorial(2 * n) for n in range(11)]
    sin_k = [(-1) ** n * w ** (2 * n + 1) / math.factorial(2 * n + 1) for n in range(10)]
    c = jnp.full_like(t, cos_k[-1])
    for k in cos_k[-2::-1]:
        c = c * t + k
    s = jnp.full_like(t, sin_k[-1])
    for k in sin_k[-2::-1]:
        s = s * t + k
    return c, s * r


def far_field_kernel(
    th_hbm, ph_hbm, p_hbm, out_ref, unit_ref,
    th_ref, ph_ref, pv, wr, wi, t_ref, acc_ref, tc_ref, ts_ref, cz_ref, sz_ref, idx_sems, sems,
):
    _, comps, gx, ny, nz = pv.shape
    half = gx // 2
    dirs = out_ref.shape[1]
    f32, bf16 = jnp.float32, jnp.bfloat16
    folded = half // XB - 1
    kb = XB * ny

    idx_copies = [
        pltpu.make_async_copy(th_hbm, th_ref, idx_sems.at[0]),
        pltpu.make_async_copy(ph_hbm, ph_ref, idx_sems.at[1]),
    ]
    for cp in idx_copies:
        cp.start()
    pieces = [[(half + 1 + XB * i, XB), (half - XB * (i + 1), XB)] for i in range(folded)]
    pieces += [[(half, 1), (gx - XB + 1, XB - 1)], [(0, XB)]]
    copies = []
    count = 0
    for group in pieces:
        made = []
        for x0, length in group:
            window = pl.ds(x0, length)
            made.append(pltpu.make_async_copy(p_hbm.at[:, :, window], pv.at[:, :, window], sems.at[count]))
            count += 1
        copies.append(made)
    chunks = len(copies)
    for made in copies[:AHEAD]:
        for cp in made:
            cp.start()

    for cp in idx_copies:
        cp.wait()
    ct, st = sincos_turns((th_ref[...].reshape(1, dirs).astype(f32) + 0.5) * (0.5 / NTHETA))
    cp_, sp_ = sincos_turns(ph_ref[...].reshape(1, dirs).astype(f32) * (1.0 / NPHI))
    unit_ref[...] = jnp.concatenate([ct, st, cp_, sp_], axis=0)
    scale = WAVE / (2.0 * math.pi)
    ux, uy, uz = scale * (st * cp_), scale * (st * sp_), scale * ct
    px = lax.broadcasted_iota(jnp.int32, tc_ref.shape, 0).astype(f32)
    c, s = sincos_turns(px * ux)
    tc_ref[...] = c.astype(bf16).astype(f32)
    ts_ref[...] = s.astype(bf16).astype(f32)
    qy = lax.broadcasted_iota(jnp.int32, (ny, dirs), 0).astype(f32) - (ny - 1) / 2.0
    cy, sy = sincos_turns(qy * uy)
    flip = 7 - lax.broadcasted_iota(jnp.int32, (2, comps, ny // 8, 8, nz), 3)

    def z_phases():
        ys, total_y = lax.axis_index("ys"), ny * lax.axis_size("ys")
        zs, total_z = lax.axis_index("zs"), nz * lax.axis_size("zs")
        y_mid = (ys * ny - total_y // 2).astype(f32) + (ny - 1) / 2.0
        z_first = (zs * nz - total_z // 2).astype(f32)
        qz = lax.broadcasted_iota(jnp.int32, (nz, dirs), 0).astype(f32) + z_first
        total = 1.0 / math.sqrt(gx * total_y * total_z)
        c, s = sincos_turns(qz * uz + y_mid * uy)
        cz_ref[...] = c * total
        sz_ref[...] = s * total

    def make_tables(chunk, slot, k0):
        for xl in range(XB):
            if chunk < folded:
                px = 1 + XB * chunk + xl
            elif chunk == folded:
                px = 0 if xl == 0 else half - XB + xl
            else:
                px = xl - half
            tc = tc_ref[pl.ds(abs(px), 1), :]
            ts = ts_ref[pl.ds(abs(px), 1), :]
            if px < 0:
                ts = -ts
            k = k0 + xl * ny
            t_ref[slot, pl.ds(k, ny), :] = (tc * cy - ts * sy).astype(bf16)
            t_ref[slot, pl.ds(kb + k, ny), :] = (ts * cy + tc * sy).astype(bf16)

    def fill(chunk, slot, k0):
        for xl in range(XB):
            k = k0 + xl * ny
            if chunk < folded:
                off = 1 + XB * chunk + xl
                p = pv[:, :, half + off].astype(f32)
                m = pv[:, :, half - off].astype(f32).reshape(2, comps, ny // 8, 8, nz)
                m = jnp.take_along_axis(m, flip, axis=3)
                m = jnp.concatenate([m[:, :, h : h + 1] for h in range(ny // 8)[::-1]], axis=2)
                m = m.reshape(2, comps, ny, nz)
                e = (p + m).astype(bf16)
                er, ei = e[0], e[1]
                oi = (p[1] - m[1]).astype(bf16)
                minus_or = (m[0] - p[0]).astype(bf16)
            else:
                x = (half if xl == 0 else gx - XB + xl) if chunk == folded else xl
                p = pv[:, :, x]
                er, ei, oi, minus_or = p[0], p[1], p[1], -p[0]
            wr[slot, :, pl.ds(k, ny), :] = er
            wi[slot, :, pl.ds(k, ny), :] = ei
            wr[slot, :, pl.ds(kb + k, ny), :] = oi
            wi[slot, :, pl.ds(kb + k, ny), :] = minus_or

    def multiply(slot, depth, block):
        a, b = 2 * block, 2 * block + 1
        w = jnp.concatenate([x[slot, i, :depth] for x in (wr, wi) for i in (a, b)], axis=1)
        return lax.dot_general(
            w, t_ref[slot, :depth], (((0,), (0,)), ((), ())), preferred_element_type=f32
        )

    firsts = [sum(GROUPS[:i]) for i in range(len(GROUPS))]

    def prepare(step):
        for n in range(GROUPS[step]):
            chunk = firsts[step] + n
            for cp in copies[chunk]:
                cp.wait()
            if chunk + AHEAD < chunks:
                for cp in copies[chunk + AHEAD]:
                    cp.start()
        for n in range(GROUPS[step]):
            chunk = firsts[step] + n
            make_tables(chunk, step % 2, 2 * kb * n)
            fill(chunk, step % 2, 2 * kb * n)

    blocks = comps // 2
    rows = 4 * nz
    prepare(0)
    for step in range(len(GROUPS)):
        depth = 2 * kb * GROUPS[step]
        last = step == len(GROUPS) - 1
        for block in range(blocks):
            g = multiply(step % 2, depth, block)
            window = pl.ds(block * rows, rows)
            if step > 0:
                g = acc_ref[window, :] + g
            if not last:
                acc_ref[window, :] = g
                if block == 0:
                    prepare(step + 1)
                    if step == 0:
                        z_phases()
            else:
                for i in range(2):
                    re = g[i * nz : (i + 1) * nz]
                    im = g[(2 + i) * nz : (3 + i) * nz]
                    cz, sz = cz_ref[...], sz_ref[...]
                    comp = 2 * block + i
                    out_ref[comp : comp + 1, :] = jnp.sum(re * cz + im * sz, axis=0, keepdims=True)
                    out_ref[comps + comp : comps + comp + 1, :] = jnp.sum(im * cz - re * sz, axis=0, keepdims=True)


def far_field(p, th, ph):
    dirs = th.shape[0]
    r, comps, gx, ny, nz = p.shape
    depth = 2 * XB * ny * max(GROUPS)
    rows = gx // 2 + 8
    hbm = pl.BlockSpec(memory_space=pltpu.HBM)
    vmem = pl.BlockSpec(memory_space=pltpu.VMEM)
    return pl.pallas_call(
        far_field_kernel,
        name="far_field",
        out_shape=(
            jax.ShapeDtypeStruct((2 * comps, dirs), jnp.float32),
            jax.ShapeDtypeStruct((4, dirs), jnp.float32),
        ),
        in_specs=[hbm, hbm, hbm],
        out_specs=(vmem, vmem),
        scratch_shapes=[
            pltpu.VMEM((dirs,), jnp.int32),
            pltpu.VMEM((dirs,), jnp.int32),
            pltpu.VMEM((r, comps, gx, ny, nz), jnp.bfloat16),
            pltpu.VMEM((2, comps, depth, nz), jnp.bfloat16),
            pltpu.VMEM((2, comps, depth, nz), jnp.bfloat16),
            pltpu.VMEM((2, depth, dirs), jnp.bfloat16),
            pltpu.VMEM((2 * comps * nz, dirs), jnp.float32),
            pltpu.VMEM((rows, dirs), jnp.float32),
            pltpu.VMEM((rows, dirs), jnp.float32),
            pltpu.VMEM((nz, dirs), jnp.float32),
            pltpu.VMEM((nz, dirs), jnp.float32),
            pltpu.SemaphoreType.DMA((2,)),
            pltpu.SemaphoreType.DMA((2 * (gx // 2 // XB) + 1,)),
        ],
        compiler_params=pltpu.CompilerParams(vmem_limit_bytes=52 * 2**20),
    )(th, ph, p)


PAULI = (((1, 0), (0, 1)), ((1, 0), (0, -1)), ((0, 1), (1, 0)), ((0, -1j), (1j, 0)))


def mueller_kernel(x_ref, m2_ref, m1_ref, mw_ref, unit_ref, o_ref):
    amplitude = (x_ref[...] + m2_ref[...]) + (m1_ref[...] + mw_ref[...])
    ct, st, cp, sp = (unit_ref[i : i + 1, :] for i in range(4))
    units = ((ct * cp, ct * sp, -st), (-sp, cp))
    re = [[None, None], [None, None]]
    im = [[None, None], [None, None]]
    for s, unit in enumerate(units):
        for p in range(2):
            a = b = 0.0
            for c, u in enumerate(unit):
                a = a + u * amplitude[3 * p + c : 3 * p + c + 1]
                b = b + u * amplitude[6 + 3 * p + c : 7 + 3 * p + c]
            re[s][p], im[s][p] = a, b
    known = {}

    def product(b, c, a, e):
        if (b, c, a, e) not in known:
            known[b, c, a, e] = (
                re[b][c] * re[a][e] + im[b][c] * im[a][e],
                im[b][c] * re[a][e] - re[b][c] * im[a][e],
            )
        return known[b, c, a, e]

    for i in range(4):
        for j in range(4):
            total = 0.0
            for a in range(2):
                for b in range(2):
                    for c in range(2):
                        for e in range(2):
                            weight = complex(PAULI[i][a][b]) * complex(PAULI[j][c][e])
                            if weight == 0:
                                continue
                            zr, zi = product(b, c, a, e)
                            if weight.real:
                                total = total + weight.real * zr
                            if weight.imag:
                                total = total - weight.imag * zi
            o_ref[4 * i + j : 4 * i + j + 1, :] = 0.5 * total


def mueller(parts, units):
    return pl.pallas_call(
        mueller_kernel,
        name="mueller",
        out_shape=jax.ShapeDtypeStruct((16, units.shape[1]), jnp.float32),
    )(*parts, units)


NEAR, WRAP, FAR = (1, 0, 3, 2), (3, 2, 1, 0), (2, 3, 0, 1)


def ring_partners(x, axis, inner):
    size = lax.axis_size(axis)

    def moved(pairing):
        def partner(i):
            at = i // inner % 4
            return i + (pairing[at] - at) * inner

        return lax.ppermute(x, axis, [(i, partner(i)) for i in range(size)])

    near, wrap, far = moved(NEAR), moved(WRAP), moved(FAR)
    return x, far, near, wrap


def ring_sum(x, axis, inner):
    own, far, near, wrap = ring_partners(x, axis, inner)
    return (own + far) + (near + wrap)


def body(polarization, theta_index, phi_index):
    x, units = far_field(polarization, theta_index, phi_index)
    x = x + lax.ppermute(x, "zs", [(i, i ^ 1) for i in range(lax.axis_size("zs"))])
    x = ring_sum(x, "zs", 2)
    x = ring_sum(x, "ys", 1)
    return mueller(ring_partners(x, "ys", 4), units)


def solution(mesh):
    return jax.shard_map(
        body,
        mesh=mesh,
        in_specs=(P(None, None, None, "ys", "zs"), P(), P()),
        out_specs=P(),
        check_vma=False,
    )
```

time: 52.1 us -> 44.9 us (0.86); the launches traced: 51.8 us -> 44.1 us
  blocking collectives: 31.1 us -> 0 us
  starting transfers between devices: 0 us -> 15.4 us
  waiting for transfers between devices: 0 us -> 12.6 us
  Pallas kernels: 19.3 us -> 14 us
  local copies, waits for them, and re-layouts: 1.36 us -> 1.98 us
    all_to_all x2 -> x0, blocking collectives: 31.1 us -> none  [the longest x1 18.3 us: body(): lax.all_to_all(copies, 'ys', split_axis=0, concat_axis=0, tiled=True)]
    ppermute x0 -> x10, starting transfers between devices: none -> 15.4 us  [the longest x9 15.3 us: moved(): return lax.ppermute(x, axis, [(i, partner(i)) for i in range(size)])]
    ppermute x0 -> x10, waiting for transfers between devices: none -> 12.6 us  [the longest x9 11.4 us: moved(): return lax.ppermute(x, axis, [(i, partner(i)) for i in range(size)])]
    pallas_call x2 -> x1, Pallas kernels: 17.6 us -> 12.5 us  [far_field(): pl.pallas_call(far_field_kernel, name='far_field', out_shape=(jax.ShapeDt...]
    unnamed x4 -> x14, local copies, waits for them, and re-layouts: 1.36 us -> 1.98 us
  transfers between devices with their start and end apart: 0 -> 10, of which waited for: 0 -> 10; matrix products, arithmetic and copies ran while one was open for 0% -> 0% of each run, Pallas kernels for 0% -> 0%
where the time goes in v2:
time: 44.9 us; the launch traced here: 44.1 us
  starting transfers between devices  15.4 us (34%)
  Pallas kernels  14 us (31%)
  waiting for transfers between devices  12.6 us (28%)
  local copies, waits for them, and re-layouts  1.98 us (4%)
    ppermute x9, starting transfers between devices, moved(): return lax.ppermute(x, axis, [(i, partner(i)) for i in range(size)])  15.3 us
    pallas_call x1, Pallas kernels, far_field(): pl.pallas_call(far_field_kernel, name='far_field', out_shape=(jax.ShapeDt...  12.5 us
    ppermute x9, waiting for transfers between devices, moved(): return lax.ppermute(x, axis, [(i, partner(i)) for i in range(size)])  11.4 us
    unnamed x14, local copies, waits for them, and re-layouts  1.98 us
    pallas_call x1, Pallas kernels, mueller(): pl.pallas_call(mueller_kernel, name='mueller', out_shape=jax.ShapeDtypeSt...  1.46 us
    ppermute x1, waiting for transfers between devices, body(): lax.ppermute(x, 'zs', [(i, i ^ 1) for i in range(lax.axis_size('zs'))])  1.19 us
  transfers between devices with their start and end apart: 10, of which 10 were waited for; matrix products, arithmetic and copies ran while one was open for 0% of the time, Pallas kernels for 0%

profile of v2, /device:TPU:0, one launch (start us, length us, event | category | flops | bytes accessed | tf_op | source)
XLA Modules:
  0.0 44.1 jit_solution(8472807525021616864)
XLA Ops:
  0.0 0.0 copy-start.1
  0.0 0.7 %copy-done.1 = s32[512]{0:T(512)S(1)} copy-done((s32[512]{0:T(512)S(1)}, s32[512]{0:T(512)}, u32[]{:S(2)}) %copy-start.1) | copy-done | bytes 2072
  0.7 0.7 %copy-done.2 = s32[512]{0:T(512)S(1)} copy-done((s32[512]{0:T(512)S(1)}, s32[512]{0:T(512)}, u32[]{:S(2)}) %copy-start.2) | copy-done | bytes 2072
  1.4 12.5 %far_field.1 = (f32[12,512]{1,0:T(8,128)S(1)}, f32[4,512]{1,0:T(4,128)S(1)}) custom-call(s32[512]{0:T(512)S(1)} %copy-done.1, s32[512]{0:T(512)S(1)} %copy-done.2, bf16[2,6,256,16,128]{4,3,2,1,0:T(8,128)(2,1)} %p_hbm.1), custom_call_target="tpu_custom_call" | custom-call | tf_op jit(solution)/shard_map/far_field/pallas_call | solution.py:187
  13.9 0.0 copy-start
  13.9 0.1 collective-permute-start
  14.0 1.2 %collective-permute-done = f32[12,512]{1,0:T(8,128)S(1)} collective-permute-done((f32[12,512]{1,0:T(8,128)S(1)}, f32[12,512]{1,0:T(8,128)S(1)}, u32[]{:S(2)}, u32[]{:S(2)}) %collective-permute-start) | collective-permute-done | bytes 24608 | tf_op jit(solution)/shard_map/ppermute | solution.py:291
  15.2 0.0 copy-done
  15.2 4.2 %collective-permute-start.3 = (f32[12,512]{1,0:T(8,128)S(1)}, f32[12,512]{1,0:T(8,128)S(1)}, u32[]{:S(2)}, u32[]{:S(2)}) collective-permute-start(f32[12,512]{1,0:T(8,128)S(1)} %add.21), channel_id=1, source_target_pairs={{0,96},{16,112},{32,64},{48,80},{64,32},{80,48},{96,0},{112,16},{1... | collective-permute-start | bytes 73736 | tf_op jit(solution)/shard_map/ppermute | solution.py:278
  19.4 0.0 collective-permute-start.2
  19.4 1.6 %collective-permute-start.1 = (f32[12,512]{1,0:T(8,128)S(1)}, f32[12,512]{1,0:T(8,128)S(1)}, u32[]{:S(2)}, u32[]{:S(2)}) collective-permute-start(f32[12,512]{1,0:T(8,128)S(1)} %add.21), channel_id=1, source_target_pairs={{0,64},{16,80},{32,96},{48,112},{64,0},{80,16},{96,32},{112,48},{1... | collective-permute-start | bytes 73736 | tf_op jit(solution)/shard_map/ppermute | solution.py:278
  21.0 0.3 collective-permute-done.3
  21.3 2.0 %collective-permute-done.2 = f32[12,512]{1,0:T(8,128)S(1)} collective-permute-done((f32[12,512]{1,0:T(8,128)S(1)}, f32[12,512]{1,0:T(8,128)S(1)}, u32[]{:S(2)}, u32[]{:S(2)}) %collective-permute-start.2) | collective-permute-done | bytes 24608 | tf_op jit(solution)/shard_map/ppermute | solution.py:278
  23.3 1.5 %collective-permute-done.1 = f32[12,512]{1,0:T(8,128)S(1)} collective-permute-done((f32[12,512]{1,0:T(8,128)S(1)}, f32[12,512]{1,0:T(8,128)S(1)}, u32[]{:S(2)}, u32[]{:S(2)}) %collective-permute-start.1) | collective-permute-done | bytes 24608 | tf_op jit(solution)/shard_map/ppermute | solution.py:278
  24.8 2.8 %collective-permute-start.6 = (f32[12,512]{1,0:T(8,128)S(1)}, f32[12,512]{1,0:T(8,128)S(1)}, u32[]{:S(2)}, u32[]{:S(2)}) collective-permute-start(f32[12,512]{1,0:T(8,128)S(1)} %add_add_fusion.1), channel_id=1, source_target_pairs={{0,3},{1,2},{2,1},{3,0},{4,7},{5,6},{6,5},{7,4},{8,11},{9,10},{10,... | collective-permute-start | bytes 73736 | tf_op jit(solution)/shard_map/ppermute | solution.py:278
  27.7 0.2 collective-permute-start.5
  27.9 1.7 %collective-permute-start.4 = (f32[12,512]{1,0:T(8,128)S(1)}, f32[12,512]{1,0:T(8,128)S(1)}, u32[]{:S(2)}, u32[]{:S(2)}) collective-permute-start(f32[12,512]{1,0:T(8,128)S(1)} %add_add_fusion.1), channel_id=1, source_target_pairs={{0,2},{1,3},{2,0},{3,1},{4,6},{5,7},{6,4},{7,5},{8,10},{9,11},{10,... | collective-permute-start | bytes 73736 | tf_op jit(solution)/shard_map/ppermute | solution.py:278
  29.6 0.4 collective-permute-done.6
  30.1 1.5 %collective-permute-done.5 = f32[12,512]{1,0:T(8,128)S(1)} collective-permute-done((f32[12,512]{1,0:T(8,128)S(1)}, f32[12,512]{1,0:T(8,128)S(1)}, u32[]{:S(2)}, u32[]{:S(2)}) %collective-permute-start.5) | collective-permute-done | bytes 24608 | tf_op jit(solution)/shard_map/ppermute | solution.py:278
  31.6 1.7 %collective-permute-done.4 = f32[12,512]{1,0:T(8,128)S(1)} collective-permute-done((f32[12,512]{1,0:T(8,128)S(1)}, f32[12,512]{1,0:T(8,128)S(1)}, u32[]{:S(2)}, u32[]{:S(2)}) %collective-permute-start.4) | collective-permute-done | bytes 24608 | tf_op jit(solution)/shard_map/ppermute | solution.py:278
  33.3 0.0 copy-start.3
  33.4 3.1 %collective-permute-start.9 = (f32[12,512]{1,0:T(8,128)S(1)}, f32[12,512]{1,0:T(8,128)S(1)}, u32[]{:S(2)}, u32[]{:S(2)}) collective-permute-start(f32[12,512]{1,0:T(8,128)S(1)} %add_add_fusion.x_ref), channel_id=1, source_target_pairs={{0,12},{1,13},{2,14},{3,15},{4,8},{5,9},{6,10},{7,11},{8,4},{9,5},... | collective-permute-start | bytes 73736 | tf_op jit(solution)/shard_map/ppermute | solution.py:278
  36.4 0.1 collective-permute-start.8
  36.6 1.6 %collective-permute-start.7 = (f32[12,512]{1,0:T(8,128)S(1)}, f32[12,512]{1,0:T(8,128)S(1)}, u32[]{:S(2)}, u32[]{:S(2)}) collective-permute-start(f32[12,512]{1,0:T(8,128)S(1)} %add_add_fusion.x_ref), channel_id=1, source_target_pairs={{0,8},{1,9},{2,10},{3,11},{4,12},{5,13},{6,14},{7,15},{8,0},{9,1},... | collective-permute-start | bytes 73736 | tf_op jit(solution)/shard_map/ppermute | solution.py:278
  38.1 0.4 collective-permute-done.9.mw_ref
  38.6 1.8 %collective-permute-done.8.m1_ref = f32[12,512]{1,0:T(8,128)S(1)} collective-permute-done((f32[12,512]{1,0:T(8,128)S(1)}, f32[12,512]{1,0:T(8,128)S(1)}, u32[]{:S(2)}, u32[]{:S(2)}) %collective-permute-start.8) | collective-permute-done | bytes 24608 | tf_op jit(solution)/shard_map/ppermute | solution.py:278
  40.4 1.6 %collective-permute-done.7.m2_ref = f32[12,512]{1,0:T(8,128)S(1)} collective-permute-done((f32[12,512]{1,0:T(8,128)S(1)}, f32[12,512]{1,0:T(8,128)S(1)}, u32[]{:S(2)}, u32[]{:S(2)}) %collective-permute-start.7) | collective-permute-done | bytes 24608 | tf_op jit(solution)/shard_map/ppermute | solution.py:278
  42.0 0.0 copy-done.3
  42.0 0.0 copy-done.4
  42.0 0.0 copy-done.5
  42.0 0.6 %copy-done.6 = f32[12,512]{1,0:T(8,128)} copy-done((f32[12,512]{1,0:T(8,128)}, f32[12,512]{1,0:T(8,128)S(1)}, u32[]{:S(2)}) %copy-start.6) | copy-done | bytes 24600
  42.6 1.5 %mueller.1 = f32[16,512]{1,0:T(8,128)} custom-call(f32[12,512]{1,0:T(8,128)} %copy-done.3, f32[12,512]{1,0:T(8,128)} %copy-done.6, f32[12,512]{1,0:T(8,128)} %copy-done.5, f32[12,512]{1,0:T(8,128)} %copy-done.4, f32[4,512]{1,0:T(4,128)} %copy-done), custom_call_target="tpu_custom_call" | custom-call | tf_op jit(solution)/shard_map/mueller/pallas_call | solution.py:260
  (7 shorter events, 0.0 us)
Async XLA Ops:
  0.0 0.7 %copy-start.1 = (s32[512]{0:T(512)S(1)}, s32[512]{0:T(512)}, u32[]{:S(2)}) copy-start(s32[512]{0:T(512)} %th_hbm.1) | copy-start | bytes 6148
  0.7 0.7 %copy-start.2 = (s32[512]{0:T(512)S(1)}, s32[512]{0:T(512)}, u32[]{:S(2)}) copy-start(s32[512]{0:T(512)} %ph_hbm.1) | copy-start | bytes 6148
  13.9 1.3 %copy-start = (f32[4,512]{1,0:T(4,128)}, f32[4,512]{1,0:T(4,128)S(1)}, u32[]{:S(2)}) copy-start(f32[4,512]{1,0:T(4,128)S(1)} %get-tuple-element.8.unit_ref) | copy-start | bytes 24580
  13.9 1.3 %collective-permute-start = (f32[12,512]{1,0:T(8,128)S(1)}, f32[12,512]{1,0:T(8,128)S(1)}, u32[]{:S(2)}, u32[]{:S(2)}) collective-permute-start(f32[12,512]{1,0:T(8,128)S(1)} %get-tuple-element.7), channel_id=1, source_target_pairs={{0,16},{16,0},{32,48},{48,32},{64,80},{80,64},{96,112},{112,96},{1... | collective-permute-start | bytes 73736 | tf_op jit(solution)/shard_map/ppermute | solution.py:291
  15.2 6.1 %collective-permute-start.3 = (f32[12,512]{1,0:T(8,128)S(1)}, f32[12,512]{1,0:T(8,128)S(1)}, u32[]{:S(2)}, u32[]{:S(2)}) collective-permute-start(f32[12,512]{1,0:T(8,128)S(1)} %add.21), channel_id=1, source_target_pairs={{0,96},{16,112},{32,64},{48,80},{64,32},{80,48},{96,0},{112,16},{1... | collective-permute-start | bytes 73736 | tf_op jit(solution)/shard_map/ppermute | solution.py:278
  19.4 3.9 %collective-permute-start.2 = (f32[12,512]{1,0:T(8,128)S(1)}, f32[12,512]{1,0:T(8,128)S(1)}, u32[]{:S(2)}, u32[]{:S(2)}) collective-permute-start(f32[12,512]{1,0:T(8,128)S(1)} %add.21), channel_id=1, source_target_pairs={{0,32},{16,48},{32,0},{48,16},{64,96},{80,112},{96,64},{112,80},{1... | collective-permute-start | bytes 73736 | tf_op jit(solution)/shard_map/ppermute | solution.py:278
  19.4 5.4 %collective-permute-start.1 = (f32[12,512]{1,0:T(8,128)S(1)}, f32[12,512]{1,0:T(8,128)S(1)}, u32[]{:S(2)}, u32[]{:S(2)}) collective-permute-start(f32[12,512]{1,0:T(8,128)S(1)} %add.21), channel_id=1, source_target_pairs={{0,64},{16,80},{32,96},{48,112},{64,0},{80,16},{96,32},{112,48},{1... | collective-permute-start | bytes 73736 | tf_op jit(solution)/shard_map/ppermute | solution.py:278
  24.8 5.2 %collective-permute-start.6 = (f32[12,512]{1,0:T(8,128)S(1)}, f32[12,512]{1,0:T(8,128)S(1)}, u32[]{:S(2)}, u32[]{:S(2)}) collective-permute-start(f32[12,512]{1,0:T(8,128)S(1)} %add_add_fusion.1), channel_id=1, source_target_pairs={{0,3},{1,2},{2,1},{3,0},{4,7},{5,6},{6,5},{7,4},{8,11},{9,10},{10,... | collective-permute-start | bytes 73736 | tf_op jit(solution)/shard_map/ppermute | solution.py:278
  27.7 3.9 %collective-permute-start.5 = (f32[12,512]{1,0:T(8,128)S(1)}, f32[12,512]{1,0:T(8,128)S(1)}, u32[]{:S(2)}, u32[]{:S(2)}) collective-permute-start(f32[12,512]{1,0:T(8,128)S(1)} %add_add_fusion.1), channel_id=1, source_target_pairs={{0,1},{1,0},{2,3},{3,2},{4,5},{5,4},{6,7},{7,6},{8,9},{9,8},{10,11... | collective-permute-start | bytes 73736 | tf_op jit(solution)/shard_map/ppermute | solution.py:278
  27.9 5.4 %collective-permute-start.4 = (f32[12,512]{1,0:T(8,128)S(1)}, f32[12,512]{1,0:T(8,128)S(1)}, u32[]{:S(2)}, u32[]{:S(2)}) collective-permute-start(f32[12,512]{1,0:T(8,128)S(1)} %add_add_fusion.1), channel_id=1, source_target_pairs={{0,2},{1,3},{2,0},{3,1},{4,6},{5,7},{6,4},{7,5},{8,10},{9,11},{10,... | collective-permute-start | bytes 73736 | tf_op jit(solution)/shard_map/ppermute | solution.py:278
  33.3 8.7 %copy-start.3 = (f32[12,512]{1,0:T(8,128)}, f32[12,512]{1,0:T(8,128)S(1)}, u32[]{:S(2)}) copy-start(f32[12,512]{1,0:T(8,128)S(1)} %add_add_fusion.x_ref) | copy-start | bytes 73732
  33.4 5.2 %collective-permute-start.9 = (f32[12,512]{1,0:T(8,128)S(1)}, f32[12,512]{1,0:T(8,128)S(1)}, u32[]{:S(2)}, u32[]{:S(2)}) collective-permute-start(f32[12,512]{1,0:T(8,128)S(1)} %add_add_fusion.x_ref), channel_id=1, source_target_pairs={{0,12},{1,13},{2,14},{3,15},{4,8},{5,9},{6,10},{7,11},{8,4},{9,5},... | collective-permute-start | bytes 73736 | tf_op jit(solution)/shard_map/ppermute | solution.py:278
  36.4 3.9 %collective-permute-start.8 = (f32[12,512]{1,0:T(8,128)S(1)}, f32[12,512]{1,0:T(8,128)S(1)}, u32[]{:S(2)}, u32[]{:S(2)}) collective-permute-start(f32[12,512]{1,0:T(8,128)S(1)} %add_add_fusion.x_ref), channel_id=1, source_target_pairs={{0,4},{1,5},{2,6},{3,7},{4,0},{5,1},{6,2},{7,3},{8,12},{9,13},{10,... | collective-permute-start | bytes 73736 | tf_op jit(solution)/shard_map/ppermute | solution.py:278
  36.6 5.4 %collective-permute-start.7 = (f32[12,512]{1,0:T(8,128)S(1)}, f32[12,512]{1,0:T(8,128)S(1)}, u32[]{:S(2)}, u32[]{:S(2)}) collective-permute-start(f32[12,512]{1,0:T(8,128)S(1)} %add_add_fusion.x_ref), channel_id=1, source_target_pairs={{0,8},{1,9},{2,10},{3,11},{4,12},{5,13},{6,14},{7,15},{8,0},{9,1},... | collective-permute-start | bytes 73736 | tf_op jit(solution)/shard_map/ppermute | solution.py:278
  38.6 3.4 %copy-start.4 = (f32[12,512]{1,0:T(8,128)}, f32[12,512]{1,0:T(8,128)S(1)}, u32[]{:S(2)}) copy-start(f32[12,512]{1,0:T(8,128)S(1)} %collective-permute-done.9.mw_ref) | copy-start | bytes 73732
  40.4 1.7 %copy-start.5 = (f32[12,512]{1,0:T(8,128)}, f32[12,512]{1,0:T(8,128)S(1)}, u32[]{:S(2)}) copy-start(f32[12,512]{1,0:T(8,128)S(1)} %collective-permute-done.8.m1_ref) | copy-start | bytes 73732
  42.0 0.6 %copy-start.6 = (f32[12,512]{1,0:T(8,128)}, f32[12,512]{1,0:T(8,128)S(1)}, u32[]{:S(2)}) copy-start(f32[12,512]{1,0:T(8,128)S(1)} %collective-permute-done.7.m2_ref) | copy-start | bytes 73732

commit v3 on v2

--- a/solution.py
+++ b/solution.py
@@ -31,8 +31,8 @@
 
 
 def far_field_kernel(
-    th_hbm, ph_hbm, p_hbm, out_ref, unit_ref,
-    th_ref, ph_ref, pv, wr, wi, t_ref, acc_ref, tc_ref, ts_ref, cz_ref, sz_ref, idx_sems, sems,
+    idx_ref, p_hbm, out_ref, unit_ref,
+    pv, wr, wi, t_ref, acc_ref, tc_ref, ts_ref, cz_ref, sz_ref, mirror, sems,
 ):
     _, comps, gx, ny, nz = pv.shape
     half = gx // 2
@@ -41,14 +41,8 @@
     folded = half // XB - 1
     kb = XB * ny
 
-    idx_copies = [
-        pltpu.make_async_copy(th_hbm, th_ref, idx_sems.at[0]),
-        pltpu.make_async_copy(ph_hbm, ph_ref, idx_sems.at[1]),
-    ]
-    for cp in idx_copies:
-        cp.start()
-    pieces = [[(half + 1 + XB * i, XB), (half - XB * (i + 1), XB)] for i in range(folded)]
-    pieces += [[(half, 1), (gx - XB + 1, XB - 1)], [(0, XB)]]
+    pieces = [[(0, XB)], [(half, 1), (gx - XB + 1, XB - 1)]]
+    pieces += [[(half + 1 + XB * i, XB), (half - XB * (i + 1), XB)] for i in range(folded)]
     copies = []
     count = 0
     for group in pieces:
@@ -63,17 +57,25 @@
         for cp in made:
             cp.start()
 
-    for cp in idx_copies:
-        cp.wait()
-    ct, st = sincos_turns((th_ref[...].reshape(1, dirs).astype(f32) + 0.5) * (0.5 / NTHETA))
-    cp_, sp_ = sincos_turns(ph_ref[...].reshape(1, dirs).astype(f32) * (1.0 / NPHI))
+    ct, st = sincos_turns((idx_ref[0:1, :].astype(f32) + 0.5) * (0.5 / NTHETA))
+    cp_, sp_ = sincos_turns(idx_ref[1:2, :].astype(f32) * (1.0 / NPHI))
     unit_ref[...] = jnp.concatenate([ct, st, cp_, sp_], axis=0)
     scale = WAVE / (2.0 * math.pi)
     ux, uy, uz = scale * (st * cp_), scale * (st * sp_), scale * ct
-    px = lax.broadcasted_iota(jnp.int32, tc_ref.shape, 0).astype(f32)
-    c, s = sincos_turns(px * ux)
-    tc_ref[...] = c.astype(bf16).astype(f32)
-    ts_ref[...] = s.astype(bf16).astype(f32)
+    inner = lax.broadcasted_iota(jnp.int32, (16, dirs), 0).astype(f32)
+    outer = lax.broadcasted_iota(jnp.int32, (8, dirs), 0).astype(f32) * 16.0
+
+    def rotated(cos_in, sin_in, cos_out, sin_out, i):
+        c, s = cos_out[i : i + 1], sin_out[i : i + 1]
+        return cos_in * c - sin_in * s, sin_in * c + cos_in * s
+
+    tc_ref[0:8, :] = jnp.ones((8, dirs), f32)
+    ts_ref[0:8, :] = jnp.zeros((8, dirs), f32)
+    x_in, x_out = sincos_turns((inner + 1.0) * ux), sincos_turns(outer * ux)
+    for i in range(half // 16):
+        c, s = rotated(*x_in, *x_out, i)
+        tc_ref[8 + 16 * i : 24 + 16 * i, :] = c.astype(bf16).astype(f32)
+        ts_ref[8 + 16 * i : 24 + 16 * i, :] = s.astype(bf16).astype(f32)
     qy = lax.broadcasted_iota(jnp.int32, (ny, dirs), 0).astype(f32) - (ny - 1) / 2.0
     cy, sy = sincos_turns(qy * uy)
     flip = 7 - lax.broadcasted_iota(jnp.int32, (2, comps, ny // 8, 8, nz), 3)
@@ -83,22 +85,25 @@
         zs, total_z = lax.axis_index("zs"), nz * lax.axis_size("zs")
         y_mid = (ys * ny - total_y // 2).astype(f32) + (ny - 1) / 2.0
         z_first = (zs * nz - total_z // 2).astype(f32)
-        qz = lax.broadcasted_iota(jnp.int32, (nz, dirs), 0).astype(f32) + z_first
         total = 1.0 / math.sqrt(gx * total_y * total_z)
-        c, s = sincos_turns(qz * uz + y_mid * uy)
-        cz_ref[...] = c * total
-        sz_ref[...] = s * total
+        c, s = sincos_turns((inner + z_first) * uz + y_mid * uy)
+        z_in, z_out = (c * total, s * total), sincos_turns(outer * uz)
+        for i in range(nz // 16):
+            c, s = rotated(*z_in, *z_out, i)
+            cz_ref[16 * i : 16 * i + 16, :] = c
+            sz_ref[16 * i : 16 * i + 16, :] = s
 
     def make_tables(chunk, slot, k0):
         for xl in range(XB):
-            if chunk < folded:
-                px = 1 + XB * chunk + xl
-            elif chunk == folded:
+            if chunk == 0:
+                px = xl - half
+            elif chunk == 1:
                 px = 0 if xl == 0 else half - XB + xl
             else:
-                px = xl - half
-            tc = tc_ref[pl.ds(abs(px), 1), :]
-            ts = ts_ref[pl.ds(abs(px), 1), :]
+                px = 1 + XB * (chunk - 2) + xl
+            row = abs(px) + 7 if px else 0
+            tc = tc_ref[pl.ds(row, 1), :]
+            ts = ts_ref[pl.ds(row, 1), :]
             if px < 0:
                 ts = -ts
             k = k0 + xl * ny
@@ -108,19 +113,17 @@
     def fill(chunk, slot, k0):
         for xl in range(XB):
             k = k0 + xl * ny
-            if chunk < folded:
-                off = 1 + XB * chunk + xl
-                p = pv[:, :, half + off].astype(f32)
+            if chunk >= 2:
+                off = 1 + XB * (chunk - 2) + xl
+                p = pv[:, :, half + off]
                 m = pv[:, :, half - off].astype(f32).reshape(2, comps, ny // 8, 8, nz)
                 m = jnp.take_along_axis(m, flip, axis=3)
                 m = jnp.concatenate([m[:, :, h : h + 1] for h in range(ny // 8)[::-1]], axis=2)
-                m = m.reshape(2, comps, ny, nz)
-                e = (p + m).astype(bf16)
-                er, ei = e[0], e[1]
-                oi = (p[1] - m[1]).astype(bf16)
-                minus_or = (m[0] - p[0]).astype(bf16)
+                mirror[off % 2] = m.reshape(2, comps, ny, nz).astype(bf16)
+                m = mirror[off % 2]
+                er, ei, oi, minus_or = p[0] + m[0], p[1] + m[1], p[1] - m[1], m[0] - p[0]
             else:
-                x = (half if xl == 0 else gx - XB + xl) if chunk == folded else xl
+                x = (half if xl == 0 else gx - XB + xl) if chunk else xl
                 p = pv[:, :, x]
                 er, ei, oi, minus_or = p[0], p[1], p[1], -p[0]
             wr[slot, :, pl.ds(k, ny), :] = er
@@ -179,6 +182,7 @@
 
 def far_field(p, th, ph):
     dirs = th.shape[0]
+    idx = jnp.stack([th, ph])
     r, comps, gx, ny, nz = p.shape
     depth = 2 * XB * ny * max(GROUPS)
     rows = gx // 2 + 8
@@ -191,11 +195,9 @@
             jax.ShapeDtypeStruct((2 * comps, dirs), jnp.float32),
             jax.ShapeDtypeStruct((4, dirs), jnp.float32),
         ),
-        in_specs=[hbm, hbm, hbm],
+        in_specs=[vmem, hbm],
         out_specs=(vmem, vmem),
         scratch_shapes=[
-            pltpu.VMEM((dirs,), jnp.int32),
-            pltpu.VMEM((dirs,), jnp.int32),
             pltpu.VMEM((r, comps, gx, ny, nz), jnp.bfloat16),
             pltpu.VMEM((2, comps, depth, nz), jnp.bfloat16),
             pltpu.VMEM((2, comps, depth, nz), jnp.bfloat16),
@@ -205,11 +207,11 @@
             pltpu.VMEM((rows, dirs), jnp.float32),
             pltpu.VMEM((nz, dirs), jnp.float32),
             pltpu.VMEM((nz, dirs), jnp.float32),
-            pltpu.SemaphoreType.DMA((2,)),
+            pltpu.VMEM((2, r, comps, ny, nz), jnp.bfloat16),
             pltpu.SemaphoreType.DMA((2 * (gx // 2 // XB) + 1,)),
         ],
         compiler_params=pltpu.CompilerParams(vmem_limit_bytes=52 * 2**20),
-    )(th, ph, p)
+    )(idx, p)
 
 
 PAULI = (((1, 0), (0, 1)), ((1, 0), (0, -1)), ((0, 1), (1, 0)), ((0, -1j), (1j, 0)))
@@ -261,6 +263,9 @@
         mueller_kernel,
         name="mueller",
         out_shape=jax.ShapeDtypeStruct((16, units.shape[1]), jnp.float32),
+        in_specs=[pl.BlockSpec(memory_space=pltpu.VMEM)] * 5,
+        out_specs=pl.BlockSpec(memory_space=pltpu.VMEM),
+        compiler_params=pltpu.CompilerParams(vmem_limit_bytes=4 * 2**20),
     )(*parts, units)
 
 

time: 44.9 us -> 42.3 us (0.942)
  local copies, waits for them, and re-layouts: 1.98 us -> 0 us
  Pallas kernels: 14 us -> 12.8 us
  other arithmetic: 0.03 us -> 0.74 us
    unnamed x14 -> x0, local copies, waits for them, and re-layouts: 1.98 us -> none
    pallas_call x1, Pallas kernels: 1.46 us -> 0.65 us  [mueller(): pl.pallas_call(mueller_kernel, name='mueller', out_shape=jax.ShapeDtypeSt...]
    another operation x0 -> x1, other arithmetic: none -> 0.71 us  [far_field(): idx = jnp.stack([th, ph])]
where the time goes in v3:
time: 42.3 us; the launch traced here: 41.5 us
  starting transfers between devices  15.3 us (36%)
  Pallas kernels  12.8 us (30%)
  waiting for transfers between devices  12.6 us (30%)
  other arithmetic  0.74 us (2%)
    ppermute x9, starting transfers between devices, moved(): return lax.ppermute(x, axis, [(i, partner(i)) for i in range(size)])  15.3 us
    pallas_call x1, Pallas kernels, far_field(): pl.pallas_call(far_field_kernel, name='far_field', out_shape=(jax.ShapeDt...  12.1 us
    ppermute x9, waiting for transfers between devices, moved(): return lax.ppermute(x, axis, [(i, partner(i)) for i in range(size)])  11.4 us
    ppermute x1, waiting for transfers between devices, body(): lax.ppermute(x, 'zs', [(i, i ^ 1) for i in range(lax.axis_size('zs'))])  1.19 us
  transfers between devices with their start and end apart: 10, of which 10 were waited for; matrix products, arithmetic and copies ran while one was open for 0% of the time, Pallas kernels for 0%

profile of v3, /device:TPU:0, one launch (start us, length us, event | category | flops | bytes accessed | tf_op | source)
XLA Modules:
  0.0 41.5 jit_solution(11443519166286638035)
XLA Ops:
  0.0 0.7 %pad_add_fusion.idx_ref = s32[2,512]{1,0:T(2,128)S(1)} fusion(s32[1,512]{1,0:T(1,128)} %bitcast.2, s32[1,512]{1,0:T(1,128)} %bitcast.3), kind=kLoop, calls=%fused_computation.2 | loop fusion | flops 1024 | bytes 8192 | tf_op jit(solution)/shard_map/stack | solution.py:185
  0.7 12.1 %far_field.1 = (f32[12,512]{1,0:T(8,128)S(1)}, f32[4,512]{1,0:T(4,128)S(1)}) custom-call(s32[2,512]{1,0:T(2,128)S(1)} %pad_add_fusion.idx_ref, bf16[2,6,256,16,128]{4,3,2,1,0:T(8,128)(2,1)} %p_hbm.1), custom_call_target="tpu_custom_call" | custom-call | tf_op jit(solution)/shard_map/far_field/pallas_call | solution.py:191
  12.8 0.1 collective-permute-start
  12.9 1.2 %collective-permute-done = f32[12,512]{1,0:T(8,128)S(1)} collective-permute-done((f32[12,512]{1,0:T(8,128)S(1)}, f32[12,512]{1,0:T(8,128)S(1)}, u32[]{:S(2)}, u32[]{:S(2)}) %collective-permute-start) | collective-permute-done | bytes 24608 | tf_op jit(solution)/shard_map/ppermute | solution.py:296
  14.1 4.2 %collective-permute-start.3 = (f32[12,512]{1,0:T(8,128)S(1)}, f32[12,512]{1,0:T(8,128)S(1)}, u32[]{:S(2)}, u32[]{:S(2)}) collective-permute-start(f32[12,512]{1,0:T(8,128)S(1)} %add.21), channel_id=1, source_target_pairs={{0,96},{16,112},{32,64},{48,80},{64,32},{80,48},{96,0},{112,16},{1... | collective-permute-start | bytes 73736 | tf_op jit(solution)/shard_map/ppermute | solution.py:283
  18.3 0.0 collective-permute-start.2
  18.3 1.5 %collective-permute-start.1 = (f32[12,512]{1,0:T(8,128)S(1)}, f32[12,512]{1,0:T(8,128)S(1)}, u32[]{:S(2)}, u32[]{:S(2)}) collective-permute-start(f32[12,512]{1,0:T(8,128)S(1)} %add.21), channel_id=1, source_target_pairs={{0,64},{16,80},{32,96},{48,112},{64,0},{80,16},{96,32},{112,48},{1... | collective-permute-start | bytes 73736 | tf_op jit(solution)/shard_map/ppermute | solution.py:283
  19.8 0.3 collective-permute-done.3
  20.2 2.0 %collective-permute-done.2 = f32[12,512]{1,0:T(8,128)S(1)} collective-permute-done((f32[12,512]{1,0:T(8,128)S(1)}, f32[12,512]{1,0:T(8,128)S(1)}, u32[]{:S(2)}, u32[]{:S(2)}) %collective-permute-start.2) | collective-permute-done | bytes 24608 | tf_op jit(solution)/shard_map/ppermute | solution.py:283
  22.2 1.5 %collective-permute-done.1 = f32[12,512]{1,0:T(8,128)S(1)} collective-permute-done((f32[12,512]{1,0:T(8,128)S(1)}, f32[12,512]{1,0:T(8,128)S(1)}, u32[]{:S(2)}, u32[]{:S(2)}) %collective-permute-start.1) | collective-permute-done | bytes 24608 | tf_op jit(solution)/shard_map/ppermute | solution.py:283
  23.7 2.8 %collective-permute-start.6 = (f32[12,512]{1,0:T(8,128)S(1)}, f32[12,512]{1,0:T(8,128)S(1)}, u32[]{:S(2)}, u32[]{:S(2)}) collective-permute-start(f32[12,512]{1,0:T(8,128)S(1)} %add_add_fusion.1), channel_id=1, source_target_pairs={{0,3},{1,2},{2,1},{3,0},{4,7},{5,6},{6,5},{7,4},{8,11},{9,10},{10,... | collective-permute-start | bytes 73736 | tf_op jit(solution)/shard_map/ppermute | solution.py:283
  26.6 0.2 collective-permute-start.5
  26.8 1.7 %collective-permute-start.4 = (f32[12,512]{1,0:T(8,128)S(1)}, f32[12,512]{1,0:T(8,128)S(1)}, u32[]{:S(2)}, u32[]{:S(2)}) collective-permute-start(f32[12,512]{1,0:T(8,128)S(1)} %add_add_fusion.1), channel_id=1, source_target_pairs={{0,2},{1,3},{2,0},{3,1},{4,6},{5,7},{6,4},{7,5},{8,10},{9,11},{10,... | collective-permute-start | bytes 73736 | tf_op jit(solution)/shard_map/ppermute | solution.py:283
  28.5 0.4 %collective-permute-done.6 = f32[12,512]{1,0:T(8,128)S(1)} collective-permute-done((f32[12,512]{1,0:T(8,128)S(1)}, f32[12,512]{1,0:T(8,128)S(1)}, u32[]{:S(2)}, u32[]{:S(2)}) %collective-permute-start.6) | collective-permute-done | bytes 24608 | tf_op jit(solution)/shard_map/ppermute | solution.py:283
  28.9 1.5 %collective-permute-done.5 = f32[12,512]{1,0:T(8,128)S(1)} collective-permute-done((f32[12,512]{1,0:T(8,128)S(1)}, f32[12,512]{1,0:T(8,128)S(1)}, u32[]{:S(2)}, u32[]{:S(2)}) %collective-permute-start.5) | collective-permute-done | bytes 24608 | tf_op jit(solution)/shard_map/ppermute | solution.py:283
  30.5 1.7 %collective-permute-done.4 = f32[12,512]{1,0:T(8,128)S(1)} collective-permute-done((f32[12,512]{1,0:T(8,128)S(1)}, f32[12,512]{1,0:T(8,128)S(1)}, u32[]{:S(2)}, u32[]{:S(2)}) %collective-permute-start.4) | collective-permute-done | bytes 24608 | tf_op jit(solution)/shard_map/ppermute | solution.py:283
  32.2 3.1 %collective-permute-start.9 = (f32[12,512]{1,0:T(8,128)S(1)}, f32[12,512]{1,0:T(8,128)S(1)}, u32[]{:S(2)}, u32[]{:S(2)}) collective-permute-start(f32[12,512]{1,0:T(8,128)S(1)} %add_add_fusion.x_ref), channel_id=1, source_target_pairs={{0,12},{1,13},{2,14},{3,15},{4,8},{5,9},{6,10},{7,11},{8,4},{9,5},... | collective-permute-start | bytes 73736 | tf_op jit(solution)/shard_map/ppermute | solution.py:283
  35.3 0.1 collective-permute-start.8
  35.5 1.5 %collective-permute-start.7 = (f32[12,512]{1,0:T(8,128)S(1)}, f32[12,512]{1,0:T(8,128)S(1)}, u32[]{:S(2)}, u32[]{:S(2)}) collective-permute-start(f32[12,512]{1,0:T(8,128)S(1)} %add_add_fusion.x_ref), channel_id=1, source_target_pairs={{0,8},{1,9},{2,10},{3,11},{4,12},{5,13},{6,14},{7,15},{8,0},{9,1},... | collective-permute-start | bytes 73736 | tf_op jit(solution)/shard_map/ppermute | solution.py:283
  37.0 0.4 %collective-permute-done.9.mw_ref = f32[12,512]{1,0:T(8,128)S(1)} collective-permute-done((f32[12,512]{1,0:T(8,128)S(1)}, f32[12,512]{1,0:T(8,128)S(1)}, u32[]{:S(2)}, u32[]{:S(2)}) %collective-permute-start.9) | collective-permute-done | bytes 24608 | tf_op jit(solution)/shard_map/ppermute | solution.py:283
  37.4 1.8 %collective-permute-done.8.m1_ref = f32[12,512]{1,0:T(8,128)S(1)} collective-permute-done((f32[12,512]{1,0:T(8,128)S(1)}, f32[12,512]{1,0:T(8,128)S(1)}, u32[]{:S(2)}, u32[]{:S(2)}) %collective-permute-start.8) | collective-permute-done | bytes 24608 | tf_op jit(solution)/shard_map/ppermute | solution.py:283
  39.2 1.6 %collective-permute-done.7.m2_ref = f32[12,512]{1,0:T(8,128)S(1)} collective-permute-done((f32[12,512]{1,0:T(8,128)S(1)}, f32[12,512]{1,0:T(8,128)S(1)}, u32[]{:S(2)}, u32[]{:S(2)}) %collective-permute-start.7) | collective-permute-done | bytes 24608 | tf_op jit(solution)/shard_map/ppermute | solution.py:283
  40.9 0.7 %mueller.1 = f32[16,512]{1,0:T(8,128)} custom-call(f32[12,512]{1,0:T(8,128)S(1)} %add_add_fusion.x_ref, f32[12,512]{1,0:T(8,128)S(1)} %collective-permute-done.7.m2_ref, f32[12,512]{1,0:T(8,128)S(1)} %collective-permute-done.8.m1_ref, f32[12,512]{1,0:T(8,128)S(1)} %collective-permute-done.9.mw_ref, f32[4,512]{1,0:T(4,128)S(1)} %get-tuple-element.8.unit_ref), custom_call_target="tpu_custom_call" | custom-call | tf_op jit(solution)/shard_map/mueller/pallas_call | solution.py:262
  (3 shorter events, 0.0 us)
Async XLA Ops:
  12.8 1.3 %collective-permute-start = (f32[12,512]{1,0:T(8,128)S(1)}, f32[12,512]{1,0:T(8,128)S(1)}, u32[]{:S(2)}, u32[]{:S(2)}) collective-permute-start(f32[12,512]{1,0:T(8,128)S(1)} %get-tuple-element.7), channel_id=1, source_target_pairs={{0,16},{16,0},{32,48},{48,32},{64,80},{80,64},{96,112},{112,96},{1... | collective-permute-start | bytes 73736 | tf_op jit(solution)/shard_map/ppermute | solution.py:296
  14.1 6.0 %collective-permute-start.3 = (f32[12,512]{1,0:T(8,128)S(1)}, f32[12,512]{1,0:T(8,128)S(1)}, u32[]{:S(2)}, u32[]{:S(2)}) collective-permute-start(f32[12,512]{1,0:T(8,128)S(1)} %add.21), channel_id=1, source_target_pairs={{0,96},{16,112},{32,64},{48,80},{64,32},{80,48},{96,0},{112,16},{1... | collective-permute-start | bytes 73736 | tf_op jit(solution)/shard_map/ppermute | solution.py:283
  18.3 3.9 %collective-permute-start.2 = (f32[12,512]{1,0:T(8,128)S(1)}, f32[12,512]{1,0:T(8,128)S(1)}, u32[]{:S(2)}, u32[]{:S(2)}) collective-permute-start(f32[12,512]{1,0:T(8,128)S(1)} %add.21), channel_id=1, source_target_pairs={{0,32},{16,48},{32,0},{48,16},{64,96},{80,112},{96,64},{112,80},{1... | collective-permute-start | bytes 73736 | tf_op jit(solution)/shard_map/ppermute | solution.py:283
  18.3 5.4 %collective-permute-start.1 = (f32[12,512]{1,0:T(8,128)S(1)}, f32[12,512]{1,0:T(8,128)S(1)}, u32[]{:S(2)}, u32[]{:S(2)}) collective-permute-start(f32[12,512]{1,0:T(8,128)S(1)} %add.21), channel_id=1, source_target_pairs={{0,64},{16,80},{32,96},{48,112},{64,0},{80,16},{96,32},{112,48},{1... | collective-permute-start | bytes 73736 | tf_op jit(solution)/shard_map/ppermute | solution.py:283
  23.7 5.2 %collective-permute-start.6 = (f32[12,512]{1,0:T(8,128)S(1)}, f32[12,512]{1,0:T(8,128)S(1)}, u32[]{:S(2)}, u32[]{:S(2)}) collective-permute-start(f32[12,512]{1,0:T(8,128)S(1)} %add_add_fusion.1), channel_id=1, source_target_pairs={{0,3},{1,2},{2,1},{3,0},{4,7},{5,6},{6,5},{7,4},{8,11},{9,10},{10,... | collective-permute-start | bytes 73736 | tf_op jit(solution)/shard_map/ppermute | solution.py:283
  26.6 3.9 %collective-permute-start.5 = (f32[12,512]{1,0:T(8,128)S(1)}, f32[12,512]{1,0:T(8,128)S(1)}, u32[]{:S(2)}, u32[]{:S(2)}) collective-permute-start(f32[12,512]{1,0:T(8,128)S(1)} %add_add_fusion.1), channel_id=1, source_target_pairs={{0,1},{1,0},{2,3},{3,2},{4,5},{5,4},{6,7},{7,6},{8,9},{9,8},{10,11... | collective-permute-start | bytes 73736 | tf_op jit(solution)/shard_map/ppermute | solution.py:283
  26.8 5.4 %collective-permute-start.4 = (f32[12,512]{1,0:T(8,128)S(1)}, f32[12,512]{1,0:T(8,128)S(1)}, u32[]{:S(2)}, u32[]{:S(2)}) collective-permute-start(f32[12,512]{1,0:T(8,128)S(1)} %add_add_fusion.1), channel_id=1, source_target_pairs={{0,2},{1,3},{2,0},{3,1},{4,6},{5,7},{6,4},{7,5},{8,10},{9,11},{10,... | collective-permute-start | bytes 73736 | tf_op jit(solution)/shard_map/ppermute | solution.py:283
  32.2 5.2 %collective-permute-start.9 = (f32[12,512]{1,0:T(8,128)S(1)}, f32[12,512]{1,0:T(8,128)S(1)}, u32[]{:S(2)}, u32[]{:S(2)}) collective-permute-start(f32[12,512]{1,0:T(8,128)S(1)} %add_add_fusion.x_ref), channel_id=1, source_target_pairs={{0,12},{1,13},{2,14},{3,15},{4,8},{5,9},{6,10},{7,11},{8,4},{9,5},... | collective-permute-start | bytes 73736 | tf_op jit(solution)/shard_map/ppermute | solution.py:283
  35.3 3.9 %collective-permute-start.8 = (f32[12,512]{1,0:T(8,128)S(1)}, f32[12,512]{1,0:T(8,128)S(1)}, u32[]{:S(2)}, u32[]{:S(2)}) collective-permute-start(f32[12,512]{1,0:T(8,128)S(1)} %add_add_fusion.x_ref), channel_id=1, source_target_pairs={{0,4},{1,5},{2,6},{3,7},{4,0},{5,1},{6,2},{7,3},{8,12},{9,13},{10,... | collective-permute-start | bytes 73736 | tf_op jit(solution)/shard_map/ppermute | solution.py:283
  35.5 5.4 %collective-permute-start.7 = (f32[12,512]{1,0:T(8,128)S(1)}, f32[12,512]{1,0:T(8,128)S(1)}, u32[]{:S(2)}, u32[]{:S(2)}) collective-permute-start(f32[12,512]{1,0:T(8,128)S(1)} %add_add_fusion.x_ref), channel_id=1, source_target_pairs={{0,8},{1,9},{2,10},{3,11},{4,12},{5,13},{6,14},{7,15},{8,0},{9,1},... | collective-permute-start | bytes 73736 | tf_op jit(solution)/shard_map/ppermute | solution.py:283

commit v4 on v3

--- a/solution.py
+++ b/solution.py
@@ -32,7 +32,7 @@
 
 def far_field_kernel(
     idx_ref, p_hbm, out_ref, unit_ref,
-    pv, wr, wi, t_ref, acc_ref, tc_ref, ts_ref, cz_ref, sz_ref, mirror, sems,
+    pv, wr, wi, t_ref, acc_ref, tc_ref, ts_ref, cz_ref, sz_ref, sems,
 ):
     _, comps, gx, ny, nz = pv.shape
     half = gx // 2
@@ -115,13 +115,15 @@
             k = k0 + xl * ny
             if chunk >= 2:
                 off = 1 + XB * (chunk - 2) + xl
-                p = pv[:, :, half + off]
+                p = pv[:, :, half + off].astype(f32)
                 m = pv[:, :, half - off].astype(f32).reshape(2, comps, ny // 8, 8, nz)
                 m = jnp.take_along_axis(m, flip, axis=3)
                 m = jnp.concatenate([m[:, :, h : h + 1] for h in range(ny // 8)[::-1]], axis=2)
-                mirror[off % 2] = m.reshape(2, comps, ny, nz).astype(bf16)
-                m = mirror[off % 2]
-                er, ei, oi, minus_or = p[0] + m[0], p[1] + m[1], p[1] - m[1], m[0] - p[0]
+                m = m.reshape(2, comps, ny, nz)
+                e = (p + m).astype(bf16)
+                er, ei = e[0], e[1]
+                oi = (p[1] - m[1]).astype(bf16)
+                minus_or = (m[0] - p[0]).astype(bf16)
             else:
                 x = (half if xl == 0 else gx - XB + xl) if chunk else xl
                 p = pv[:, :, x]
@@ -207,7 +209,6 @@
             pltpu.VMEM((rows, dirs), jnp.float32),
             pltpu.VMEM((nz, dirs), jnp.float32),
             pltpu.VMEM((nz, dirs), jnp.float32),
-            pltpu.VMEM((2, r, comps, ny, nz), jnp.bfloat16),
             pltpu.SemaphoreType.DMA((2 * (gx // 2 // XB) + 1,)),
         ],
         compiler_params=pltpu.CompilerParams(vmem_limit_bytes=52 * 2**20),

time: 42.3 us -> 41.7 us (0.986)
  Pallas kernels: 12.8 us -> 12.2 us
    pallas_call x1, Pallas kernels: 12.1 us -> 11.6 us  [far_field(): pl.pallas_call(far_field_kernel, name='far_field', out_shape=(jax.ShapeDt...]
where the time goes in v4:
time: 41.7 us; the launch traced here: 41 us
  starting transfers between devices  15.3 us (37%)
  waiting for transfers between devices  12.6 us (30%)
  Pallas kernels  12.2 us (29%)
  other arithmetic  0.74 us (2%)
    ppermute x9, starting transfers between devices, moved(): return lax.ppermute(x, axis, [(i, partner(i)) for i in range(size)])  15.3 us
    pallas_call x1, Pallas kernels, far_field(): pl.pallas_call(far_field_kernel, name='far_field', out_shape=(jax.ShapeDt...  11.6 us
    ppermute x9, waiting for transfers between devices, moved(): return lax.ppermute(x, axis, [(i, partner(i)) for i in range(size)])  11.4 us
    ppermute x1, waiting for transfers between devices, body(): lax.ppermute(x, 'zs', [(i, i ^ 1) for i in range(lax.axis_size('zs'))])  1.19 us
  transfers between devices with their start and end apart: 10, of which 10 were waited for; matrix products, arithmetic and copies ran while one was open for 0% of the time, Pallas kernels for 0%

profile of v4, /device:TPU:0, one launch (start us, length us, event | category | flops | bytes accessed | tf_op | source)
XLA Modules:
  0.0 41.0 jit_solution(16964149134444565768)
XLA Ops:
  0.0 0.7 %pad_add_fusion.idx_ref = s32[2,512]{1,0:T(2,128)S(1)} fusion(s32[1,512]{1,0:T(1,128)} %bitcast.2, s32[1,512]{1,0:T(1,128)} %bitcast.3), kind=kLoop, calls=%fused_computation.2 | loop fusion | flops 1024 | bytes 8192 | tf_op jit(solution)/shard_map/stack | solution.py:187
  0.7 11.6 %far_field.1 = (f32[12,512]{1,0:T(8,128)S(1)}, f32[4,512]{1,0:T(4,128)S(1)}) custom-call(s32[2,512]{1,0:T(2,128)S(1)} %pad_add_fusion.idx_ref, bf16[2,6,256,16,128]{4,3,2,1,0:T(8,128)(2,1)} %p_hbm.1), custom_call_target="tpu_custom_call" | custom-call | tf_op jit(solution)/shard_map/far_field/pallas_call | solution.py:193
  12.3 0.1 collective-permute-start
  12.4 1.2 %collective-permute-done = f32[12,512]{1,0:T(8,128)S(1)} collective-permute-done((f32[12,512]{1,0:T(8,128)S(1)}, f32[12,512]{1,0:T(8,128)S(1)}, u32[]{:S(2)}, u32[]{:S(2)}) %collective-permute-start) | collective-permute-done | bytes 24608 | tf_op jit(solution)/shard_map/ppermute | solution.py:297
  13.6 4.1 %collective-permute-start.3 = (f32[12,512]{1,0:T(8,128)S(1)}, f32[12,512]{1,0:T(8,128)S(1)}, u32[]{:S(2)}, u32[]{:S(2)}) collective-permute-start(f32[12,512]{1,0:T(8,128)S(1)} %add.21), channel_id=1, source_target_pairs={{0,96},{16,112},{32,64},{48,80},{64,32},{80,48},{96,0},{112,16},{1... | collective-permute-start | bytes 73736 | tf_op jit(solution)/shard_map/ppermute | solution.py:284
  17.8 0.0 collective-permute-start.2
  17.8 1.5 %collective-permute-start.1 = (f32[12,512]{1,0:T(8,128)S(1)}, f32[12,512]{1,0:T(8,128)S(1)}, u32[]{:S(2)}, u32[]{:S(2)}) collective-permute-start(f32[12,512]{1,0:T(8,128)S(1)} %add.21), channel_id=1, source_target_pairs={{0,64},{16,80},{32,96},{48,112},{64,0},{80,16},{96,32},{112,48},{1... | collective-permute-start | bytes 73736 | tf_op jit(solution)/shard_map/ppermute | solution.py:284
  19.3 0.3 collective-permute-done.3
  19.6 2.0 %collective-permute-done.2 = f32[12,512]{1,0:T(8,128)S(1)} collective-permute-done((f32[12,512]{1,0:T(8,128)S(1)}, f32[12,512]{1,0:T(8,128)S(1)}, u32[]{:S(2)}, u32[]{:S(2)}) %collective-permute-start.2) | collective-permute-done | bytes 24608 | tf_op jit(solution)/shard_map/ppermute | solution.py:284
  21.7 1.5 %collective-permute-done.1 = f32[12,512]{1,0:T(8,128)S(1)} collective-permute-done((f32[12,512]{1,0:T(8,128)S(1)}, f32[12,512]{1,0:T(8,128)S(1)}, u32[]{:S(2)}, u32[]{:S(2)}) %collective-permute-start.1) | collective-permute-done | bytes 24608 | tf_op jit(solution)/shard_map/ppermute | solution.py:284
  23.2 2.8 %collective-permute-start.6 = (f32[12,512]{1,0:T(8,128)S(1)}, f32[12,512]{1,0:T(8,128)S(1)}, u32[]{:S(2)}, u32[]{:S(2)}) collective-permute-start(f32[12,512]{1,0:T(8,128)S(1)} %add_add_fusion.1), channel_id=1, source_target_pairs={{0,3},{1,2},{2,1},{3,0},{4,7},{5,6},{6,5},{7,4},{8,11},{9,10},{10,... | collective-permute-start | bytes 73736 | tf_op jit(solution)/shard_map/ppermute | solution.py:284
  26.0 0.2 collective-permute-start.5
  26.3 1.7 %collective-permute-start.4 = (f32[12,512]{1,0:T(8,128)S(1)}, f32[12,512]{1,0:T(8,128)S(1)}, u32[]{:S(2)}, u32[]{:S(2)}) collective-permute-start(f32[12,512]{1,0:T(8,128)S(1)} %add_add_fusion.1), channel_id=1, source_target_pairs={{0,2},{1,3},{2,0},{3,1},{4,6},{5,7},{6,4},{7,5},{8,10},{9,11},{10,... | collective-permute-start | bytes 73736 | tf_op jit(solution)/shard_map/ppermute | solution.py:284
  28.0 0.4 %collective-permute-done.6 = f32[12,512]{1,0:T(8,128)S(1)} collective-permute-done((f32[12,512]{1,0:T(8,128)S(1)}, f32[12,512]{1,0:T(8,128)S(1)}, u32[]{:S(2)}, u32[]{:S(2)}) %collective-permute-start.6) | collective-permute-done | bytes 24608 | tf_op jit(solution)/shard_map/ppermute | solution.py:284
  28.4 1.5 %collective-permute-done.5 = f32[12,512]{1,0:T(8,128)S(1)} collective-permute-done((f32[12,512]{1,0:T(8,128)S(1)}, f32[12,512]{1,0:T(8,128)S(1)}, u32[]{:S(2)}, u32[]{:S(2)}) %collective-permute-start.5) | collective-permute-done | bytes 24608 | tf_op jit(solution)/shard_map/ppermute | solution.py:284
  29.9 1.7 %collective-permute-done.4 = f32[12,512]{1,0:T(8,128)S(1)} collective-permute-done((f32[12,512]{1,0:T(8,128)S(1)}, f32[12,512]{1,0:T(8,128)S(1)}, u32[]{:S(2)}, u32[]{:S(2)}) %collective-permute-start.4) | collective-permute-done | bytes 24608 | tf_op jit(solution)/shard_map/ppermute | solution.py:284
  31.7 3.1 %collective-permute-start.9 = (f32[12,512]{1,0:T(8,128)S(1)}, f32[12,512]{1,0:T(8,128)S(1)}, u32[]{:S(2)}, u32[]{:S(2)}) collective-permute-start(f32[12,512]{1,0:T(8,128)S(1)} %add_add_fusion.x_ref), channel_id=1, source_target_pairs={{0,12},{1,13},{2,14},{3,15},{4,8},{5,9},{6,10},{7,11},{8,4},{9,5},... | collective-permute-start | bytes 73736 | tf_op jit(solution)/shard_map/ppermute | solution.py:284
  34.8 0.1 collective-permute-start.8
  34.9 1.5 %collective-permute-start.7 = (f32[12,512]{1,0:T(8,128)S(1)}, f32[12,512]{1,0:T(8,128)S(1)}, u32[]{:S(2)}, u32[]{:S(2)}) collective-permute-start(f32[12,512]{1,0:T(8,128)S(1)} %add_add_fusion.x_ref), channel_id=1, source_target_pairs={{0,8},{1,9},{2,10},{3,11},{4,12},{5,13},{6,14},{7,15},{8,0},{9,1},... | collective-permute-start | bytes 73736 | tf_op jit(solution)/shard_map/ppermute | solution.py:284
  36.5 0.4 %collective-permute-done.9.mw_ref = f32[12,512]{1,0:T(8,128)S(1)} collective-permute-done((f32[12,512]{1,0:T(8,128)S(1)}, f32[12,512]{1,0:T(8,128)S(1)}, u32[]{:S(2)}, u32[]{:S(2)}) %collective-permute-start.9) | collective-permute-done | bytes 24608 | tf_op jit(solution)/shard_map/ppermute | solution.py:284
  36.9 1.8 %collective-permute-done.8.m1_ref = f32[12,512]{1,0:T(8,128)S(1)} collective-permute-done((f32[12,512]{1,0:T(8,128)S(1)}, f32[12,512]{1,0:T(8,128)S(1)}, u32[]{:S(2)}, u32[]{:S(2)}) %collective-permute-start.8) | collective-permute-done | bytes 24608 | tf_op jit(solution)/shard_map/ppermute | solution.py:284
  38.7 1.6 %collective-permute-done.7.m2_ref = f32[12,512]{1,0:T(8,128)S(1)} collective-permute-done((f32[12,512]{1,0:T(8,128)S(1)}, f32[12,512]{1,0:T(8,128)S(1)}, u32[]{:S(2)}, u32[]{:S(2)}) %collective-permute-start.7) | collective-permute-done | bytes 24608 | tf_op jit(solution)/shard_map/ppermute | solution.py:284
  40.3 0.7 %mueller.1 = f32[16,512]{1,0:T(8,128)} custom-call(f32[12,512]{1,0:T(8,128)S(1)} %add_add_fusion.x_ref, f32[12,512]{1,0:T(8,128)S(1)} %collective-permute-done.7.m2_ref, f32[12,512]{1,0:T(8,128)S(1)} %collective-permute-done.8.m1_ref, f32[12,512]{1,0:T(8,128)S(1)} %collective-permute-done.9.mw_ref, f32[4,512]{1,0:T(4,128)S(1)} %get-tuple-element.8.unit_ref), custom_call_target="tpu_custom_call" | custom-call | tf_op jit(solution)/shard_map/mueller/pallas_call | solution.py:263
  (3 shorter events, 0.0 us)
Async XLA Ops:
  12.3 1.3 %collective-permute-start = (f32[12,512]{1,0:T(8,128)S(1)}, f32[12,512]{1,0:T(8,128)S(1)}, u32[]{:S(2)}, u32[]{:S(2)}) collective-permute-start(f32[12,512]{1,0:T(8,128)S(1)} %get-tuple-element.7), channel_id=1, source_target_pairs={{0,16},{16,0},{32,48},{48,32},{64,80},{80,64},{96,112},{112,96},{1... | collective-permute-start | bytes 73736 | tf_op jit(solution)/shard_map/ppermute | solution.py:297
  13.6 6.0 %collective-permute-start.3 = (f32[12,512]{1,0:T(8,128)S(1)}, f32[12,512]{1,0:T(8,128)S(1)}, u32[]{:S(2)}, u32[]{:S(2)}) collective-permute-start(f32[12,512]{1,0:T(8,128)S(1)} %add.21), channel_id=1, source_target_pairs={{0,96},{16,112},{32,64},{48,80},{64,32},{80,48},{96,0},{112,16},{1... | collective-permute-start | bytes 73736 | tf_op jit(solution)/shard_map/ppermute | solution.py:284
  17.8 3.9 %collective-permute-start.2 = (f32[12,512]{1,0:T(8,128)S(1)}, f32[12,512]{1,0:T(8,128)S(1)}, u32[]{:S(2)}, u32[]{:S(2)}) collective-permute-start(f32[12,512]{1,0:T(8,128)S(1)} %add.21), channel_id=1, source_target_pairs={{0,32},{16,48},{32,0},{48,16},{64,96},{80,112},{96,64},{112,80},{1... | collective-permute-start | bytes 73736 | tf_op jit(solution)/shard_map/ppermute | solution.py:284
  17.8 5.4 %collective-permute-start.1 = (f32[12,512]{1,0:T(8,128)S(1)}, f32[12,512]{1,0:T(8,128)S(1)}, u32[]{:S(2)}, u32[]{:S(2)}) collective-permute-start(f32[12,512]{1,0:T(8,128)S(1)} %add.21), channel_id=1, source_target_pairs={{0,64},{16,80},{32,96},{48,112},{64,0},{80,16},{96,32},{112,48},{1... | collective-permute-start | bytes 73736 | tf_op jit(solution)/shard_map/ppermute | solution.py:284
  23.2 5.2 %collective-permute-start.6 = (f32[12,512]{1,0:T(8,128)S(1)}, f32[12,512]{1,0:T(8,128)S(1)}, u32[]{:S(2)}, u32[]{:S(2)}) collective-permute-start(f32[12,512]{1,0:T(8,128)S(1)} %add_add_fusion.1), channel_id=1, source_target_pairs={{0,3},{1,2},{2,1},{3,0},{4,7},{5,6},{6,5},{7,4},{8,11},{9,10},{10,... | collective-permute-start | bytes 73736 | tf_op jit(solution)/shard_map/ppermute | solution.py:284
  26.0 3.9 %collective-permute-start.5 = (f32[12,512]{1,0:T(8,128)S(1)}, f32[12,512]{1,0:T(8,128)S(1)}, u32[]{:S(2)}, u32[]{:S(2)}) collective-permute-start(f32[12,512]{1,0:T(8,128)S(1)} %add_add_fusion.1), channel_id=1, source_target_pairs={{0,1},{1,0},{2,3},{3,2},{4,5},{5,4},{6,7},{7,6},{8,9},{9,8},{10,11... | collective-permute-start | bytes 73736 | tf_op jit(solution)/shard_map/ppermute | solution.py:284
  26.3 5.4 %collective-permute-start.4 = (f32[12,512]{1,0:T(8,128)S(1)}, f32[12,512]{1,0:T(8,128)S(1)}, u32[]{:S(2)}, u32[]{:S(2)}) collective-permute-start(f32[12,512]{1,0:T(8,128)S(1)} %add_add_fusion.1), channel_id=1, source_target_pairs={{0,2},{1,3},{2,0},{3,1},{4,6},{5,7},{6,4},{7,5},{8,10},{9,11},{10,... | collective-permute-start | bytes 73736 | tf_op jit(solution)/shard_map/ppermute | solution.py:284
  31.7 5.2 %collective-permute-start.9 = (f32[12,512]{1,0:T(8,128)S(1)}, f32[12,512]{1,0:T(8,128)S(1)}, u32[]{:S(2)}, u32[]{:S(2)}) collective-permute-start(f32[12,512]{1,0:T(8,128)S(1)} %add_add_fusion.x_ref), channel_id=1, source_target_pairs={{0,12},{1,13},{2,14},{3,15},{4,8},{5,9},{6,10},{7,11},{8,4},{9,5},... | collective-permute-start | bytes 73736 | tf_op jit(solution)/shard_map/ppermute | solution.py:284
  34.8 3.9 %collective-permute-start.8 = (f32[12,512]{1,0:T(8,128)S(1)}, f32[12,512]{1,0:T(8,128)S(1)}, u32[]{:S(2)}, u32[]{:S(2)}) collective-permute-start(f32[12,512]{1,0:T(8,128)S(1)} %add_add_fusion.x_ref), channel_id=1, source_target_pairs={{0,4},{1,5},{2,6},{3,7},{4,0},{5,1},{6,2},{7,3},{8,12},{9,13},{10,... | collective-permute-start | bytes 73736 | tf_op jit(solution)/shard_map/ppermute | solution.py:284
  34.9 5.4 %collective-permute-start.7 = (f32[12,512]{1,0:T(8,128)S(1)}, f32[12,512]{1,0:T(8,128)S(1)}, u32[]{:S(2)}, u32[]{:S(2)}) collective-permute-start(f32[12,512]{1,0:T(8,128)S(1)} %add_add_fusion.x_ref), channel_id=1, source_target_pairs={{0,8},{1,9},{2,10},{3,11},{4,12},{5,13},{6,14},{7,15},{8,0},{9,1},... | collective-permute-start | bytes 73736 | tf_op jit(solution)/shard_map/ppermute | solution.py:284
